TPU v7x, 32 devices: a whole 2x2x4 slice. The times are simulated.
32 devices in a mesh: groups: 2 (over x), traces: 16 (over z, y, core).
Axes of the slice: x: 2, y: 2, z: 4, core: 2. Of those that a mesh axis runs over, the one named last changes fastest.
Arguments:
- raw_traces: float32 [8192, 8192], P(('groups', 'traces')), parts along dimension 0, may hold values from -6 to 6
- filter_index: int32 [8192], P(('groups', 'traces')), parts along dimension 0, may hold values from 0 to 255
- channel_order: int32 [512], P('groups'), parts along dimension 0, may hold values from 0 to 255, each once
- wavelets: float32 [256, 256], P('traces'), may hold values from -0.375 to 0.375
- damping: float32 [256], P('traces'), may hold values from 0.02 to 0.5
Outputs:
- deconvolved: float32 [8192, 8192], P(('groups', 'traces')), parts along dimension 0
There are 2 independent parts, one for each index of `groups`. A program takes and returns all parts, laid end to end along the dimension named above; an argument that names none is the same for every part. Nothing has to cross between parts.
Inputs may be any that keep to these rules, and one draw needn't show every extreme that they name: `channel_order`: each of 0 to 255 appears once.
All inputs are finite; a program needn't handle non-finite values.
Results may differ from a plain program's by a relative error of at most 0.00021.
Values sent between devices are 32-bit elements; how exact they have to be, the bound alone decides.
A program may use at most 192 MiB of HBM per device.

v0:
```python
import functools
import math

import jax
import jax.numpy as jnp
import numpy as np
from jax import lax
from jax.experimental import pallas as pl
from jax.experimental.pallas import tpu as pltpu
from jax.sharding import PartitionSpec as P

LANES = 128
RADIX = 8
ROWS = 16
SUBLANES = 8

KEPT = (
    [RADIX * b for b in range(RADIX // 2 + 1)]
    + [a + RADIX * b for a in range(1, RADIX // 2) for b in range(RADIX)]
    + [RADIX // 2 + RADIX * b for b in range(RADIX // 2)]
)
SLOT = {k: s for s, k in enumerate(KEPT)}
KEEP = len(KEPT)


def lane_matrix(sign, scale):
    ids = np.arange(LANES)
    angle = 2.0 * np.pi * (np.outer(ids, ids) % LANES) / LANES
    c, s = np.cos(angle) * scale, sign * np.sin(angle) * scale
    full = np.block([[c, s], [-s, c]])
    import ml_dtypes

    high = full.astype(np.float32).astype(ml_dtypes.bfloat16)
    low = (full.astype(np.float32) - high.astype(np.float32)).astype(ml_dtypes.bfloat16)
    return np.concatenate([high, high, low], axis=0)


def twiddles(length, taps):
    m = np.arange(LANES)
    rows = []
    for k in KEPT:
        angle = 2.0 * np.pi * k * m / length
        row = [np.cos(angle), -np.sin(angle)]
        weight = 1.0 if k in (0, RADIX * RADIX // 2) else 2.0
        row += [weight * np.cos(angle), weight * np.sin(angle)]
        for piece in range(taps // LANES):
            shifted = 2.0 * np.pi * k * (m + LANES * piece) / length
            row += [np.cos(shifted), -np.sin(shifted)]
        rows.append(np.stack(row))
    return np.stack(rows).astype(np.float32)


def cadd(a, b):
    return (a[0] + b[0], a[1] + b[1])


def csub(a, b):
    return (a[0] - b[0], a[1] - b[1])


def turn(a, num, den):
    num %= den
    if num == 0:
        return a
    if 4 * num == den:
        return (-a[1], a[0])
    if 2 * num == den:
        return (-a[0], -a[1])
    if 4 * num == 3 * den:
        return (a[1], -a[0])
    c, s = math.cos(2 * math.pi * num / den), math.sin(2 * math.pi * num / den)
    return (a[0] * c - a[1] * s, a[0] * s + a[1] * c)


def fourier(items, sign):
    n = len(items)
    if n == 1:
        return items
    even, odd = fourier(items[0::2], sign), fourier(items[1::2], sign)
    turned = [turn(o, sign * k, n) for k, o in enumerate(odd)]
    return [cadd(e, t) for e, t in zip(even, turned)] + [csub(e, t) for e, t in zip(even, turned)]


def real_eight(v):
    h = math.sqrt(0.5)
    s0, d0, s1, d1 = v[0] + v[4], v[0] - v[4], v[1] + v[5], v[1] - v[5]
    s2, d2, s3, d3 = v[2] + v[6], v[2] - v[6], v[3] + v[7], v[3] - v[7]
    p, q = s0 + s2, s1 + s3
    r, t = (d1 - d3) * h, (d1 + d3) * h
    return [p + q, (d0 + r, -(d2 + t)), (s0 - s2, s3 - s1), (d0 - r, d2 - t), p - q]


def eight_real(u0, u1, u2, u3, u4):
    h = math.sqrt(0.5)
    p, q = u0 + u4, u0 - u4
    e = [p + u2[0], q - u2[1], p - u2[0], q + u2[1]]
    f, g = u1[0] - u3[0], u1[1] + u3[1]
    o = [u1[0] + u3[0], (f - g) * h, u3[1] - u1[1], -(f + g) * h]
    return [a + b for a, b in zip(e, o)] + [a - b for a, b in zip(e, o)]


def put_split(ref, base, re, im):
    rows = pl.ds(base, ROWS)
    for part, value in enumerate((re, im)):
        high = value.astype(jnp.bfloat16)
        low = (value - high.astype(jnp.float32)).astype(jnp.bfloat16)
        at = part * LANES
        ref[rows, at : at + LANES] = high
        ref[rows, 2 * LANES + at : 2 * LANES + at + LANES] = low
        ref[rows, 4 * LANES + at : 4 * LANES + at + LANES] = high


def deconvolve(read, write, wave, floor, fwd_ref, inv_ref, tw_ref, mid_ref, cut_ref, spec_ref):
    half, wide = RADIX // 2, RADIX * RADIX
    for j2 in range(RADIX):
        out = real_eight([read(RADIX * j1 + j2) for j1 in range(RADIX)])
        mid_ref[2 * j2] = out[0]
        mid_ref[2 * j2 + 1] = out[half]
        for a in range(1, half):
            mid_ref[2 * RADIX * a + 2 * j2] = out[a][0]
            mid_ref[2 * RADIX * a + 2 * j2 + 1] = out[a][1]

    def emit(k, value):
        s = SLOT[k]
        c, n = tw_ref[s, 0:1, :], tw_ref[s, 1:2, :]
        put_split(cut_ref, s * ROWS, value[0] * c - value[1] * n, value[0] * n + value[1] * c)

    zero = real_eight([mid_ref[2 * j2] for j2 in range(RADIX)])
    c, n = tw_ref[0, 0:1, :], tw_ref[0, 1:2, :]
    for b in range(half + 1):
        s = SLOT[RADIX * b]
        c, n = tw_ref[s, 0:1, :], tw_ref[s, 1:2, :]
        if b in (0, half):
            put_split(cut_ref, s * ROWS, zero[b] * c, zero[b] * n)
        else:
            emit(RADIX * b, zero[b])
    for a in range(1, half):
        base = 2 * RADIX * a
        items = [turn((mid_ref[base + 2 * j2], mid_ref[base + 2 * j2 + 1]), -a * j2, wide) for j2 in range(RADIX)]
        for b, value in enumerate(fourier(items, -1)):
            emit(a + RADIX * b, value)
    four = [mid_ref[2 * j2 + 1] for j2 in range(RADIX)]
    for b in range(half):
        k = half + RADIX * b
        re, im = four[0], None
        for j2 in range(1, RADIX):
            angle = 2 * math.pi * (k * j2 % wide) / wide
            re = re + four[j2] * math.cos(angle)
            term = four[j2] * -math.sin(angle)
            im = term if im is None else im + term
        emit(k, (re, im))

    for s in range(KEEP):
        re = im = None
        for piece, taps in enumerate(wave):
            c, n = tw_ref[s, 4 + 2 * piece : 5 + 2 * piece, :], tw_ref[s, 5 + 2 * piece : 6 + 2 * piece, :]
            re = taps * c if re is None else re + taps * c
            im = taps * n if im is None else im + taps * n
        put_split(cut_ref, (KEEP + s) * ROWS, re, im)

    spec_ref[...] = jnp.dot(cut_ref[...], fwd_ref[...], preferred_element_type=jnp.float32)

    def apply(s, carry):
        at = pl.multiple_of(s * ROWS, ROWS)
        other = pl.multiple_of((KEEP + s) * ROWS, ROWS)
        xr, xi = spec_ref[pl.ds(at, ROWS), 0:LANES], spec_ref[pl.ds(at, ROWS), LANES:]
        hr, hi = spec_ref[pl.ds(other, ROWS), 0:LANES], spec_ref[pl.ds(other, ROWS), LANES:]
        scale = 1.0 / (hr * hr + hi * hi + floor)
        put_split(cut_ref, at, (xr * hr + xi * hi) * scale, (xi * hr - xr * hi) * scale)
        return carry

    lax.fori_loop(0, KEEP, apply, 0, unroll=3)
    rows = KEEP * ROWS
    spec_ref[0:rows] = jnp.dot(cut_ref[0:rows], inv_ref[...], preferred_element_type=jnp.float32)

    def fetch(k):
        s = SLOT[k]
        re, im = spec_ref[s * ROWS : (s + 1) * ROWS, 0:LANES], spec_ref[s * ROWS : (s + 1) * ROWS, LANES:]
        c, n = tw_ref[s, 2:3, :], tw_ref[s, 3:4, :]
        if k in (0, wide // 2):
            return re * c - im * n
        return (re * c - im * n, re * n + im * c)

    for a in range(1, half):
        base = 2 * RADIX * a
        for j2, value in enumerate(fourier([fetch(a + RADIX * b) for b in range(RADIX)], 1)):
            value = turn(value, a * j2, wide)
            mid_ref[base + 2 * j2] = value[0]
            mid_ref[base + 2 * j2 + 1] = value[1]
    for j2, value in enumerate(eight_real(*[fetch(RADIX * b) for b in range(half + 1)])):
        mid_ref[2 * j2] = value
    four = [fetch(half + RADIX * b) for b in range(half)]
    for j2 in range(RADIX):
        total = None
        for b, value in enumerate(four):
            angle = 2 * math.pi * ((half + RADIX * b) * j2 % wide) / wide
            term = value[0] * math.cos(angle)
            if j2:
                term = term - value[1] * math.sin(angle)
            total = term if total is None else total + term
        mid_ref[2 * j2 + 1] = total
    for j2 in range(RADIX):
        parts = [mid_ref[2 * j2]]
        for a in range(1, half):
            base = 2 * RADIX * a
            parts.append((mid_ref[base + 2 * j2], mid_ref[base + 2 * j2 + 1]))
        parts.append(mid_ref[2 * j2 + 1])
        for j1, value in enumerate(eight_real(*parts)):
            write(RADIX * j1 + j2, value)


def slabs(ref, lead):
    def at(j):
        return lead + (slice(None), slice(j * LANES, (j + 1) * LANES))

    def read(j):
        value = ref[at(j)]
        return value.reshape(ROWS, LANES)

    def write(j, value):
        ref[at(j)] = value.reshape(ref[at(j)].shape)

    return read, write


def block_kernel(taps, lead, x_ref, w_ref, fwd_ref, inv_ref, tw_ref, o_ref, mid_ref, cut_ref, spec_ref):
    read, _ = slabs(x_ref, lead)
    _, write = slabs(o_ref, (slice(None),) * (len(o_ref.shape) - 2))
    wave = [w_ref[:, p * LANES : (p + 1) * LANES] for p in range(taps // LANES)]
    deconvolve(read, write, wave, w_ref[:, taps : taps + LANES], fwd_ref, inv_ref, tw_ref, mid_ref, cut_ref, spec_ref)


def place_kernel(taps, row_ref, x_ref, w_ref, fwd_ref, inv_ref, tw_ref, o_ref, mid_ref, cut_ref, spec_ref, res_ref, sems):
    step, steps = pl.program_id(0), pl.num_programs(0)
    slot = lax.rem(step, 2)

    def rows_of(at, slot, act):
        for r in range(ROWS):
            copy = pltpu.make_async_copy(
                res_ref.at[slot, pl.ds(r, 1)], o_ref.at[pl.ds(row_ref[at * ROWS + r], 1)], sems.at[slot, r]
            )
            act(copy)

    @pl.when(step >= 2)
    def _():
        rows_of(step - 2, slot, lambda copy: copy.wait())

    read, _ = slabs(x_ref, (slice(None),) * (len(x_ref.shape) - 2))

    def write(j, value):
        res_ref[slot, :, j * LANES : (j + 1) * LANES] = value

    wave = [w_ref[:, p * LANES : (p + 1) * LANES] for p in range(taps // LANES)]
    deconvolve(read, write, wave, w_ref[:, taps : taps + LANES], fwd_ref, inv_ref, tw_ref, mid_ref, cut_ref, spec_ref)
    rows_of(step, slot, lambda copy: copy.start())

    @pl.when(step == steps - 1)
    def _():
        @pl.when(step >= 1)
        def _():
            rows_of(step - 1, 1 - slot, lambda copy: copy.wait())

        rows_of(step, slot, lambda copy: copy.wait())


def settle_kernel(row_ref, came_ref, filled_ref, o_ref, held_ref, in_sems, out_sems):
    del filled_ref
    blocks, rows, _ = came_ref.shape

    def take(d):
        return pltpu.make_async_copy(came_ref.at[d], held_ref.at[d], in_sems.at[d])

    def put(d, r):
        return pltpu.make_async_copy(
            held_ref.at[d, pl.ds(r, 1)], o_ref.at[pl.ds(row_ref[d * rows + r], 1)], out_sems.at[d, r]
        )

    for d in range(blocks):
        take(d).start()

    def send(d, carry):
        take(d).wait()
        for r in range(rows):
            put(d, r).start()
        return carry

    lax.fori_loop(0, blocks, send, 0)

    def finish(d, carry):
        for r in range(rows):
            put(d, r).wait()
        return carry

    lax.fori_loop(0, blocks, finish, 0)


def tables(length, taps):
    return (
        jnp.asarray(lane_matrix(-1.0, 1.0)),
        jnp.asarray(lane_matrix(1.0, 1.0 / length)),
        jnp.asarray(twiddles(length, taps)),
    )


def scratch():
    return [
        pltpu.VMEM((RADIX * RADIX, ROWS, LANES), jnp.float32),
        pltpu.VMEM((2 * KEEP * ROWS, 6 * LANES), jnp.bfloat16),
        pltpu.VMEM((2 * KEEP * ROWS, 2 * LANES), jnp.float32),
    ]


def local(raw_traces, filter_index, channel_order, wavelets, damping):
    rows, length = raw_traces.shape
    own, taps = wavelets.shape
    n = lax.axis_size("traces")
    me = lax.axis_index("traces")
    each = rows // n
    floor = damping * (jnp.sum(wavelets * wavelets, axis=1) + 1e-6)
    picks = filter_index.reshape(own, rows // own).astype(jnp.float32)
    packed = lax.all_gather(jnp.concatenate([wavelets, floor[:, None], picks], axis=1), "traces", axis=0, tiled=True)
    part = each // 2
    first = raw_traces.reshape(n, each, length)[:, :part]
    first, packed = lax.optimization_barrier((first, packed))
    all_picks = packed[:, taps + 1 :].reshape(n, n, each).astype(jnp.int32)
    came_picks = lax.dynamic_index_in_dim(all_picks, me, 1, keepdims=False)
    bank = jnp.concatenate([packed[:, :taps], jnp.broadcast_to(packed[:, taps : taps + 1], (own * n, LANES))], axis=1)
    fwd, inv, tw = tables(length, taps)
    whole = lambda a: pl.BlockSpec(a.shape, lambda i, *_: (0,) * a.ndim)
    fixed = [pl.BlockSpec((ROWS, taps + LANES), lambda i, *_: (i, 0)), whole(fwd), whole(inv), whole(tw)]
    params = pltpu.CompilerParams(vmem_limit_bytes=48 * 1024 * 1024)
    places = (jnp.arange(each)[None, :] * n + jnp.arange(n)[:, None]).reshape(-1)

    if each % (2 * SUBLANES):
        came = lax.all_to_all(raw_traces.reshape(n, each, length), "traces", 0, 0, tiled=True).reshape(rows, length)
        result = pl.pallas_call(
            functools.partial(block_kernel, taps, ()),
            grid=(rows // ROWS,),
            out_shape=jax.ShapeDtypeStruct((rows, length), jnp.float32),
            in_specs=[pl.BlockSpec((ROWS, length), lambda i: (i, 0))] + fixed,
            out_specs=pl.BlockSpec((ROWS, length), lambda i: (i, 0)),
            scratch_shapes=scratch(),
            compiler_params=params,
        )(came, jnp.take(bank, came_picks.reshape(-1), axis=0), fwd, inv, tw)
        return jnp.take(result, (channel_order % n) * each + channel_order // n, axis=0)

    hits = channel_order[None, :] == places[:, None]
    row_of = jnp.sum(jnp.where(hits, jnp.arange(rows)[None, :], 0), axis=1).reshape(n, 2, each // 2)
    group = ROWS // part if part < ROWS else 1
    split = raw_traces.reshape(n, 2, part, length)
    steps = n // group
    flops = pl.CostEstimate(flops=steps * ROWS * length * 1500, bytes_accessed=8 * steps * ROWS * length, transcendentals=0)

    came_raw = lax.all_to_all(first, "traces", 0, 0, tiled=True)
    own_rows = filter_index.reshape(n, 2, part)[:, 1].reshape(-1)
    done_here = pl.pallas_call(
        functools.partial(block_kernel, taps, (slice(None), 0)),
        grid=(steps,),
        out_shape=jax.ShapeDtypeStruct((n, part, length), jnp.float32),
        in_specs=[pl.BlockSpec((group, 1, part, length), lambda i: (i, 1, 0, 0))] + fixed,
        out_specs=pl.BlockSpec((group, part, length), lambda i: (i, 0, 0)),
        scratch_shapes=scratch(),
        compiler_params=params,
        cost_estimate=flops,
    )(split, jnp.take(bank, own_rows, axis=0), fwd, inv, tw)
    came_done = lax.all_to_all(done_here, "traces", 0, 0, tiled=True)
    came_rows = came_picks[:, :part].reshape(-1)
    filled = pl.pallas_call(
        functools.partial(place_kernel, taps),
        grid_spec=pltpu.PrefetchScalarGridSpec(
            num_scalar_prefetch=1,
            grid=(steps,),
            in_specs=[pl.BlockSpec((group, part, length), lambda i, *_: (i, 0, 0))] + fixed,
            out_specs=pl.BlockSpec(memory_space=pl.ANY),
            scratch_shapes=scratch()
            + [pltpu.VMEM((2, ROWS, length), jnp.float32), pltpu.SemaphoreType.DMA((2, ROWS))],
        ),
        out_shape=jax.ShapeDtypeStruct((rows, length), jnp.float32),
        compiler_params=params,
        cost_estimate=flops,
    )(row_of[:, 0].reshape(-1), came_raw, jnp.take(bank, came_rows, axis=0), fwd, inv, tw)
    return pl.pallas_call(
        settle_kernel,
        in_specs=[pl.BlockSpec(memory_space=pltpu.SMEM)] + [pl.BlockSpec(memory_space=pl.ANY)] * 2,
        out_specs=pl.BlockSpec(memory_space=pl.ANY),
        out_shape=jax.ShapeDtypeStruct((rows, length), jnp.float32),
        scratch_shapes=[
            pltpu.VMEM((n, part, length), jnp.float32),
            pltpu.SemaphoreType.DMA((n,)),
            pltpu.SemaphoreType.DMA((n, part)),
        ],
        input_output_aliases={2: 0},
        compiler_params=params,
    )(row_of[:, 1].reshape(-1), came_done, filled)


def solution(mesh):
    placed = (
        P(("groups", "traces"), None),
        P(("groups", "traces")),
        P("groups"),
        P("traces", None),
        P("traces"),
    )
    return jax.shard_map(
        local, mesh=mesh, in_specs=placed, out_specs=P(("groups", "traces"), None), check_vma=False
    )
```

profile of v0, /device:TPU:16, one launch (start us, length us, event | category | flops | bytes accessed | tf_op | source)
XLA Modules:
  0.0 230.5 jit_solution(5791961086968669960)
XLA Ops:
  0.0 0.8 multiply_reduce_fusion
  0.8 0.7 convert_element_type.12
  1.6 0.7 multiply_bitcast_fusion
  2.3 0.1 copy.12
  2.3 0.8 pad_maximum_fusion.1
  3.1 17.1 %all_gather.3 = f32[256,273]{1,0:T(8,128)S(1)} all-gather(f32[16,273]{1,0:T(8,128)S(1)} %pad_maximum_fusion.1), channel_id=1, replica_groups=mesh['groups'=2,'traces'=16] {'traces'}, dimensions={0}, use_global_device_ids=true | all-gather | bytes 297024 | tf_op jit(solution)/shard_map/all_gather | solution.py:321
  20.2 4.6 %slice.38 = f32[16,8,8192]{2,1,0:T(8,128)} slice(f32[16,16,8192]{2,1,0:T(8,128)} %bitcast.7), slice={[0:16], [0:8], [0:8192]} | slice | bytes 8388608 | tf_op jit(solution)/shard_map/slice | solution.py:323
  24.8 10.4 %all-to-all-start.1 = ((f32[16,8,8192]{2,1,0:T(8,128)}), f32[16,8,8192]{2,1,0:T(8,128)}, u32[]{:S(2)}, u32[]{:S(2)}) async-start(f32[16,8,8192]{2,1,0:T(8,128)} %slice.38), calls=%async_computation.1 | async-start | bytes 8388608 | tf_op jit(solution)/shard_map/all_to_all | solution.py:354
  35.2 0.1 reshape.47
  35.5 0.1 slice_reduce_fusion
  35.6 0.1 broadcast_in_dim.39
  35.8 0.8 gather_fusion
  36.7 17.0 %shard_map.82 = f32[16,8,8192]{2,1,0:T(8,128)S(1)} custom-call(f32[16,2,8,8192]{3,2,1,0:T(8,128)} %bitcast.8, f32[128,384]{1,0:T(8,128)S(1)} %broadcast_select_fusion.1.w_ref, bf16[768,256]{1,0:T(8,128)(2,1)S(1)} %copy-done.2, bf16[768,256]{1,0:T(8,128)(2,1)S(1)} %copy-done.1, f32[33,8,128]{2,1,0:T(8,128)S(1)} %copy-done.3), custom_call_target="tpu_custom_call" | custom-call | flops 1572864000 | bytes 8388608 | tf_op jit(solution)/shard_map/pallas_call | solution.py:356
  53.7 2.0 copy-done
  55.7 72.2 %all-to-all-done.1.x_ref = f32[16,8,8192]{2,1,0:T(8,128)} async-done(((f32[16,8,8192]{2,1,0:T(8,128)}), f32[16,8,8192]{2,1,0:T(8,128)}, u32[]{:S(2)}, u32[]{:S(2)}) %all-to-all-start.1) | async-done | bytes 4194336 | tf_op jit(solution)/shard_map/all_to_all | solution.py:354
  127.9 4.6 %all-to-all-start = ((f32[16,8,8192]{2,1,0:T(8,128)}), f32[16,8,8192]{2,1,0:T(8,128)}, u32[]{:S(2)}, u32[]{:S(2)}) async-start(f32[16,8,8192]{2,1,0:T(8,128)} %copy-done), calls=%async_computation | async-start | bytes 8388608 | tf_op jit(solution)/shard_map/all_to_all | solution.py:366
  132.6 0.2 select_reduce_fusion
  132.8 0.1 reshape.44
  133.0 0.1 reshape_squeeze.9.row_ref
  133.1 0.1 slice_convert_fusion
  133.3 0.8 gather_fusion.1
  134.2 19.3 %shard_map.83.filled_ref = f32[256,8192]{1,0:T(8,128)} custom-call(s32[128]{0:T(128)S(1)} %reshape_squeeze.11.row_ref, f32[16,8,8192]{2,1,0:T(8,128)} %all-to-all-done.1.x_ref, f32[128,384]{1,0:T(8,128)S(1)} %broadcast_select_fusion.w_ref, bf16[768,256]{1,0:T(8,128)(2,1)S(1)} %copy-done.2, bf16[768,256]{1,0:T(8,128)(2,1)S(1)} %copy-done.1, ...), custom_call_target="tpu_custom_call" | custom-call | flops 1572864000 | bytes 8388608 | tf_op jit(solution)/shard_map/pallas_call | solution.py:368
  153.5 71.6 %all-to-all-done.came_ref = f32[16,8,8192]{2,1,0:T(8,128)} async-done(((f32[16,8,8192]{2,1,0:T(8,128)}), f32[16,8,8192]{2,1,0:T(8,128)}, u32[]{:S(2)}, u32[]{:S(2)}) %all-to-all-start) | async-done | bytes 4194336 | tf_op jit(solution)/shard_map/all_to_all | solution.py:366
  225.1 5.4 %shard_map.84 = f32[256,8192]{1,0:T(8,128)} custom-call(s32[128]{0:T(128)S(1)} %reshape_squeeze.9.row_ref, f32[16,8,8192]{2,1,0:T(8,128)} %all-to-all-done.came_ref, f32[256,8192]{1,0:T(8,128)} %shard_map.83.filled_ref), custom_call_target="tpu_custom_call", output_to_operand_aliasing={{}: (2, {})} | custom-call | tf_op jit(solution)/shard_map/pallas_call | solution.py:382
  (31 shorter events, 0.8 us)
Async XLA Ops:
  24.8 10.4 %copy-start.4 = (s32[256]{0:T(256)S(1)}, s32[256]{0:T(256)}, u32[]{:S(2)}) copy-start(s32[256]{0:T(256)} %param.11) | copy-start | bytes 3076
  24.8 11.8 %copy-start.1 = (bf16[768,256]{1,0:T(8,128)(2,1)S(1)}, bf16[768,256]{1,0:T(8,128)(2,1)}, u32[]{:S(2)}) copy-start(bf16[768,256]{1,0:T(8,128)(2,1)} %constant.15.clone.inv_ref) | copy-start | bytes 1179652
  24.8 11.8 %copy-start.2 = (bf16[768,256]{1,0:T(8,128)(2,1)S(1)}, bf16[768,256]{1,0:T(8,128)(2,1)}, u32[]{:S(2)}) copy-start(bf16[768,256]{1,0:T(8,128)(2,1)} %constant.10.clone.fwd_ref) | copy-start | bytes 1179652
  24.8 11.8 %copy-start.3 = (f32[33,8,128]{2,1,0:T(8,128)S(1)}, f32[33,8,128]{2,1,0:T(8,128)}, u32[]{:S(2)}) copy-start(f32[33,8,128]{2,1,0:T(8,128)} %constant.34.clone.tw_ref) | copy-start | bytes 405508
  24.8 103.1 %all-to-all-start.1 = ((f32[16,8,8192]{2,1,0:T(8,128)}), f32[16,8,8192]{2,1,0:T(8,128)}, u32[]{:S(2)}, u32[]{:S(2)}) async-start(f32[16,8,8192]{2,1,0:T(8,128)} %slice.38), calls=%async_computation.1 | async-start | bytes 8388608 | tf_op jit(solution)/shard_map/all_to_all | solution.py:354
  53.7 2.0 copy-start
  55.7 76.9 %copy-start.5 = (s32[256]{0:T(256)S(1)}, s32[256]{0:T(256)}, u32[]{:S(2)}) copy-start(s32[256]{0:T(256)} %param.12) | copy-start | bytes 3076
  127.9 97.2 %all-to-all-start = ((f32[16,8,8192]{2,1,0:T(8,128)}), f32[16,8,8192]{2,1,0:T(8,128)}, u32[]{:S(2)}, u32[]{:S(2)}) async-start(f32[16,8,8192]{2,1,0:T(8,128)} %copy-done), calls=%async_computation | async-start | bytes 8388608 | tf_op jit(solution)/shard_map/all_to_all | solution.py:366
where the time goes:
time: 231 us
  waiting for transfers between devices  144 us (62%)
  Pallas kernels  41.7 us (18%)
  blocking collectives  17.1 us (7%)
  starting transfers between devices  15 us (6%)
  local copies, waits for them, and re-layouts  9.22 us (4%)
  other arithmetic  3.49 us (2%)
    all_to_all x1, waiting for transfers between devices, local(): came_raw = lax.all_to_all(first, 'traces', 0, 0, tiled=True)  72.2 us
    all_to_all x1, waiting for transfers between devices, local(): came_done = lax.all_to_all(done_here, 'traces', 0, 0, tiled=True)  71.6 us
    pallas_call x1, Pallas kernels, local(): pl.pallas_call(functools.partial(place_kernel, taps), grid_spec=pltpu.Pre...  19.3 us
    all_gather x1, blocking collectives, local(): lax.all_gather(jnp.concatenate([wavelets, floor[:, None], picks], axis=1)...  17.1 us
    pallas_call x1, Pallas kernels, local(): pl.pallas_call(functools.partial(block_kernel, taps, (slice(None), 0)), g...  17 us
    all_to_all x1, starting transfers between devices, local(): came_raw = lax.all_to_all(first, 'traces', 0, 0, tiled=True)  10.4 us
    pallas_call x1, Pallas kernels, local(): pl.pallas_call(settle_kernel, in_specs=[pl.BlockSpec(memory_space=pltpu.S...  5.38 us
  transfers between devices with their start and end apart: 2, of which 2 were waited for; matrix products, arithmetic and copies ran while one was open for 1% of the time, Pallas kernels for 16%

commit v1 on v0

--- a/solution.py
+++ b/solution.py
@@ -230,68 +230,240 @@
     deconvolve(read, write, wave, w_ref[:, taps : taps + LANES], fwd_ref, inv_ref, tw_ref, mid_ref, cut_ref, spec_ref)
 
 
-def place_kernel(taps, row_ref, x_ref, w_ref, fwd_ref, inv_ref, tw_ref, o_ref, mid_ref, cut_ref, spec_ref, res_ref, sems):
-    step, steps = pl.program_id(0), pl.num_programs(0)
-    slot = lax.rem(step, 2)
-
-    def rows_of(at, slot, act):
+def split_count(n):
+    inner = 1
+    while inner * inner < n:
+        inner *= 2
+    return (n // inner, inner) if n % inner == 0 else (1, n)
+
+
+def exchange_kernel(
+    n,
+    taps,
+    x_ref,
+    pick_ref,
+    wave_ref,
+    damp_ref,
+    fwd_hbm,
+    inv_hbm,
+    tw_hbm,
+    buf_ref,
+    mid_ref,
+    cut_ref,
+    spec_ref,
+    fwd_ref,
+    inv_ref,
+    tw_ref,
+    bank_ref,
+    rows_ref,
+    pick_smem,
+    damp_smem,
+    load_sems,
+    near_sems,
+    raw_sems,
+    pick_sems,
+    bank_sends,
+    bank_recvs,
+    sends,
+    recvs,
+):
+    me = lax.axis_index("traces")
+    own, each = wave_ref.shape[0], x_ref.shape[0] // n
+    half = n // 2
+    partner = lax.rem(me + half, n)
+    outer, inner = split_count(n)
+    far, near = lax.div(me, inner), lax.rem(me, inner)
+    halves, pieces = own // SUBLANES, taps // LANES
+    last = halves * pieces
+
+    def remote(src, dst, send_sem, recv_sem, device):
+        return pltpu.make_async_remote_copy(
+            src_ref=src,
+            dst_ref=dst,
+            send_sem=send_sem,
+            recv_sem=recv_sem,
+            device_id={"traces": device},
+            device_id_type=pl.DeviceIdType.MESH,
+        )
+
+    def block_of(e):
+        return x_ref.at[pl.ds(pl.multiple_of(e * each, each), each)]
+
+    barrier = pltpu.get_barrier_semaphore()
+
+    def greet(k, carry):
+        other = lax.rem(me + k, n)
+        pl.semaphore_signal(barrier, inc=1, device_id={"traces": other}, device_id_type=pl.DeviceIdType.MESH)
+        return carry
+
+    lax.fori_loop(1, n, greet, 0)
+
+    damp_in = pltpu.make_async_copy(damp_ref, damp_smem, near_sems.at[0])
+    pick_in = pltpu.make_async_copy(pick_ref, pick_smem.at[0], near_sems.at[1])
+    tables_in = [
+        pltpu.make_async_copy(there, here, near_sems.at[2 + i])
+        for i, (there, here) in enumerate(((fwd_hbm, fwd_ref), (inv_hbm, inv_ref), (tw_hbm, tw_ref)))
+    ]
+    tiles_in = [
+        pltpu.make_async_copy(
+            wave_ref.at[pl.ds(h * SUBLANES, SUBLANES), pl.ds(p * LANES, LANES)],
+            bank_ref.at[me, h * pieces + p],
+            near_sems.at[5 + h * pieces + p],
+        )
+        for h in range(halves)
+        for p in range(pieces)
+    ]
+    for copy in [damp_in] + tiles_in + [pick_in] + tables_in:
+        copy.start()
+
+    def load(e):
+        return pltpu.make_async_copy(block_of(e), buf_ref.at[n + e], load_sems.at[e])
+
+    def load_start(k, carry):
+        @pl.when(k != half)
+        def _():
+            load(lax.rem(me + k, n)).start()
+
+        return carry
+
+    lax.fori_loop(1, n + 1, load_start, 0)
+
+    damp_in.wait()
+    lane = lax.broadcasted_iota(jnp.int32, (SUBLANES, LANES), 1)
+    levels = jnp.zeros((SUBLANES, LANES), jnp.float32)
+    for f in range(own):
+        levels = jnp.where(lane == f, damp_smem[f], levels)
+    bank_ref[me, last] = levels
+    for copy in tiles_in:
+        copy.wait()
+    pl.semaphore_wait(barrier, n - 1)
+
+    def far_copy(t):
+        there = lax.rem(far + t, outer) * inner + near
+        return remote(bank_ref.at[me], bank_ref.at[me], bank_sends.at[t - 1], bank_recvs.at[me], there)
+
+    def near_copy(t, d):
+        block = lax.rem(far + t, outer) * inner + near
+        there = far * inner + lax.rem(near + d, inner)
+        slot = outer - 1 + (d - 1) * outer + t
+        return remote(bank_ref.at[block], bank_ref.at[block], bank_sends.at[slot], bank_recvs.at[block], there)
+
+    def bank_came(block):
+        return remote(bank_ref.at[block], bank_ref.at[block], bank_sends.at[0], bank_recvs.at[block], partner)
+
+    for t in range(1, outer):
+        far_copy(t).start()
+    raw_out = remote(block_of(partner), buf_ref.at[n + me], raw_sems.at[0], raw_sems.at[1], partner)
+    raw_came = remote(block_of(partner), buf_ref.at[n + partner], raw_sems.at[0], raw_sems.at[1], partner)
+    picks_out = remote(pick_ref, pick_smem.at[1], pick_sems.at[0], pick_sems.at[1], partner)
+    raw_out.start()
+    picks_out.start()
+    for d in range(1, inner):
+        near_copy(0, d).start()
+    for t in range(1, outer):
+        bank_came(lax.rem(far + t, outer) * inner + near).wait_recv()
+        for d in range(1, inner):
+            near_copy(t, d).start()
+    for d in range(1, inner):
+        for t in range(outer):
+            bank_came(lax.rem(far + t, outer) * inner + lax.rem(near + d, inner)).wait_recv()
+    pick_in.wait()
+    for copy in tables_in:
+        copy.wait()
+
+    def turn_of(s):
+        return jnp.where(s < half - 1, s + 1, jnp.where(s < n - 2, s + 2, jnp.where(s == n - 2, half, 0)))
+
+    def send(e):
+        return remote(buf_ref.at[n + e], buf_ref.at[me], sends.at[e], recvs.at[me], e)
+
+    row_lane = lax.broadcasted_iota(jnp.int32, (1, LANES), 1)
+
+    def step(s, carry):
+        e = lax.rem(me + turn_of(s), n)
+        theirs = s == n - 2
+
+        @pl.when(theirs)
+        def _():
+            raw_came.wait_recv()
+            picks_out.wait_recv()
+
+        @pl.when(jnp.logical_not(theirs))
+        def _():
+            load(e).wait()
+
+        table = jnp.where(theirs, 1, 0)
+        base = jnp.where(theirs, me, e) * each
         for r in range(ROWS):
-            copy = pltpu.make_async_copy(
-                res_ref.at[slot, pl.ds(r, 1)], o_ref.at[pl.ds(row_ref[at * ROWS + r], 1)], sems.at[slot, r]
-            )
-            act(copy)
-
-    @pl.when(step >= 2)
-    def _():
-        rows_of(step - 2, slot, lambda copy: copy.wait())
-
-    read, _ = slabs(x_ref, (slice(None),) * (len(x_ref.shape) - 2))
-
-    def write(j, value):
-        res_ref[slot, :, j * LANES : (j + 1) * LANES] = value
-
-    wave = [w_ref[:, p * LANES : (p + 1) * LANES] for p in range(taps // LANES)]
-    deconvolve(read, write, wave, w_ref[:, taps : taps + LANES], fwd_ref, inv_ref, tw_ref, mid_ref, cut_ref, spec_ref)
-    rows_of(step, slot, lambda copy: copy.start())
-
-    @pl.when(step == steps - 1)
-    def _():
-        @pl.when(step >= 1)
+            pick = pick_smem[table, base + r]
+            block, inside = lax.div(pick, own), lax.rem(pick, own)
+            tile, sub = lax.div(inside, SUBLANES) * pieces, lax.rem(inside, SUBLANES)
+            for p in range(pieces):
+                rows_ref[r : r + 1, p * LANES : (p + 1) * LANES] = bank_ref[block, tile + p, pl.ds(sub, 1), :]
+            level = bank_ref[block, last, 0:1, :]
+            rows_ref[r : r + 1, taps : taps + LANES] = jnp.where(row_lane == inside, level, 0.0)
+
+        @pl.when(jnp.logical_and(s >= 1, s <= n - 2))
         def _():
-            rows_of(step - 1, 1 - slot, lambda copy: copy.wait())
-
-        rows_of(step, slot, lambda copy: copy.wait())
-
-
-def settle_kernel(row_ref, came_ref, filled_ref, o_ref, held_ref, in_sems, out_sems):
-    del filled_ref
-    blocks, rows, _ = came_ref.shape
-
-    def take(d):
-        return pltpu.make_async_copy(came_ref.at[d], held_ref.at[d], in_sems.at[d])
-
-    def put(d, r):
-        return pltpu.make_async_copy(
-            held_ref.at[d, pl.ds(r, 1)], o_ref.at[pl.ds(row_ref[d * rows + r], 1)], out_sems.at[d, r]
-        )
-
-    for d in range(blocks):
-        take(d).start()
-
-    def send(d, carry):
-        take(d).wait()
-        for r in range(rows):
-            put(d, r).start()
-        return carry
-
-    lax.fori_loop(0, blocks, send, 0)
+            send(lax.rem(me + turn_of(s - 1), n)).start()
+
+        slot = jnp.where(s >= n - 2, e, n + e)
+        wave = [rows_ref[:, p * LANES : (p + 1) * LANES] for p in range(pieces)]
+        power = sum(jnp.sum(w * w, axis=1, keepdims=True) for w in wave)
+        damp = jnp.sum(rows_ref[:, taps : taps + LANES], axis=1, keepdims=True)
+        floor = jnp.broadcast_to(damp * (power + 1e-6), (ROWS, LANES))
+
+        def read(j):
+            return buf_ref[n + e, :, j * LANES : (j + 1) * LANES]
+
+        def write(j, value):
+            buf_ref[slot, :, j * LANES : (j + 1) * LANES] = value
+
+        deconvolve(read, write, wave, floor, fwd_ref, inv_ref, tw_ref, mid_ref, cut_ref, spec_ref)
+        return carry
+
+    lax.fori_loop(0, n, step, 0)
+
+    raw_out.wait_send()
+    picks_out.wait_send()
+    for t in range(1, outer):
+        far_copy(t).wait_send()
+    for d in range(1, inner):
+        for t in range(outer):
+            near_copy(t, d).wait_send()
+
+    def finish(k, carry):
+        @pl.when(k != half)
+        def _():
+            e = lax.rem(me + k, n)
+            send(e).wait_send()
+            remote(buf_ref.at[e], buf_ref.at[e], sends.at[e], recvs.at[e], e).wait_recv()
+
+        return carry
+
+    lax.fori_loop(1, n, finish, 0)
+
+
+def settle_kernel(n, order_ref, came_ref, o_ref, sems):
+    rows = o_ref.shape[0]
+    each = rows // n
+
+    def put(d, carry):
+        for r in range(each):
+            q = d * each + r
+            place = order_ref[q]
+            came = came_ref.at[lax.rem(place, n), pl.ds(lax.div(place, n), 1)]
+            pltpu.make_async_copy(came, o_ref.at[pl.ds(q, 1)], sems.at[d]).start()
+        return carry
+
+    lax.fori_loop(0, n, put, 0)
 
     def finish(d, carry):
-        for r in range(rows):
-            put(d, r).wait()
-        return carry
-
-    lax.fori_loop(0, blocks, finish, 0)
+        part = o_ref.at[pl.ds(pl.multiple_of(d * each, each), each)]
+        pltpu.make_async_copy(came_ref.at[0], part, sems.at[d]).wait()
+        return carry
+
+    lax.fori_loop(0, n, finish, 0)
 
 
 def tables(length, taps):
@@ -310,7 +482,7 @@
     ]
 
 
-def local(raw_traces, filter_index, channel_order, wavelets, damping):
+def gathered(raw_traces, filter_index, channel_order, wavelets, damping):
     rows, length = raw_traces.shape
     own, taps = wavelets.shape
     n = lax.axis_size("traces")
@@ -319,79 +491,70 @@
     floor = damping * (jnp.sum(wavelets * wavelets, axis=1) + 1e-6)
     picks = filter_index.reshape(own, rows // own).astype(jnp.float32)
     packed = lax.all_gather(jnp.concatenate([wavelets, floor[:, None], picks], axis=1), "traces", axis=0, tiled=True)
-    part = each // 2
-    first = raw_traces.reshape(n, each, length)[:, :part]
-    first, packed = lax.optimization_barrier((first, packed))
     all_picks = packed[:, taps + 1 :].reshape(n, n, each).astype(jnp.int32)
     came_picks = lax.dynamic_index_in_dim(all_picks, me, 1, keepdims=False)
     bank = jnp.concatenate([packed[:, :taps], jnp.broadcast_to(packed[:, taps : taps + 1], (own * n, LANES))], axis=1)
     fwd, inv, tw = tables(length, taps)
     whole = lambda a: pl.BlockSpec(a.shape, lambda i, *_: (0,) * a.ndim)
     fixed = [pl.BlockSpec((ROWS, taps + LANES), lambda i, *_: (i, 0)), whole(fwd), whole(inv), whole(tw)]
-    params = pltpu.CompilerParams(vmem_limit_bytes=48 * 1024 * 1024)
-    places = (jnp.arange(each)[None, :] * n + jnp.arange(n)[:, None]).reshape(-1)
-
-    if each % (2 * SUBLANES):
-        came = lax.all_to_all(raw_traces.reshape(n, each, length), "traces", 0, 0, tiled=True).reshape(rows, length)
-        result = pl.pallas_call(
-            functools.partial(block_kernel, taps, ()),
-            grid=(rows // ROWS,),
-            out_shape=jax.ShapeDtypeStruct((rows, length), jnp.float32),
-            in_specs=[pl.BlockSpec((ROWS, length), lambda i: (i, 0))] + fixed,
-            out_specs=pl.BlockSpec((ROWS, length), lambda i: (i, 0)),
-            scratch_shapes=scratch(),
-            compiler_params=params,
-        )(came, jnp.take(bank, came_picks.reshape(-1), axis=0), fwd, inv, tw)
-        return jnp.take(result, (channel_order % n) * each + channel_order // n, axis=0)
-
-    hits = channel_order[None, :] == places[:, None]
-    row_of = jnp.sum(jnp.where(hits, jnp.arange(rows)[None, :], 0), axis=1).reshape(n, 2, each // 2)
-    group = ROWS // part if part < ROWS else 1
-    split = raw_traces.reshape(n, 2, part, length)
-    steps = n // group
-    flops = pl.CostEstimate(flops=steps * ROWS * length * 1500, bytes_accessed=8 * steps * ROWS * length, transcendentals=0)
-
-    came_raw = lax.all_to_all(first, "traces", 0, 0, tiled=True)
-    own_rows = filter_index.reshape(n, 2, part)[:, 1].reshape(-1)
-    done_here = pl.pallas_call(
-        functools.partial(block_kernel, taps, (slice(None), 0)),
-        grid=(steps,),
-        out_shape=jax.ShapeDtypeStruct((n, part, length), jnp.float32),
-        in_specs=[pl.BlockSpec((group, 1, part, length), lambda i: (i, 1, 0, 0))] + fixed,
-        out_specs=pl.BlockSpec((group, part, length), lambda i: (i, 0, 0)),
+    came = lax.all_to_all(raw_traces.reshape(n, each, length), "traces", 0, 0, tiled=True).reshape(rows, length)
+    result = pl.pallas_call(
+        functools.partial(block_kernel, taps, ()),
+        grid=(rows // ROWS,),
+        out_shape=jax.ShapeDtypeStruct((rows, length), jnp.float32),
+        in_specs=[pl.BlockSpec((ROWS, length), lambda i: (i, 0))] + fixed,
+        out_specs=pl.BlockSpec((ROWS, length), lambda i: (i, 0)),
         scratch_shapes=scratch(),
-        compiler_params=params,
-        cost_estimate=flops,
-    )(split, jnp.take(bank, own_rows, axis=0), fwd, inv, tw)
-    came_done = lax.all_to_all(done_here, "traces", 0, 0, tiled=True)
-    came_rows = came_picks[:, :part].reshape(-1)
-    filled = pl.pallas_call(
-        functools.partial(place_kernel, taps),
-        grid_spec=pltpu.PrefetchScalarGridSpec(
-            num_scalar_prefetch=1,
-            grid=(steps,),
-            in_specs=[pl.BlockSpec((group, part, length), lambda i, *_: (i, 0, 0))] + fixed,
-            out_specs=pl.BlockSpec(memory_space=pl.ANY),
-            scratch_shapes=scratch()
-            + [pltpu.VMEM((2, ROWS, length), jnp.float32), pltpu.SemaphoreType.DMA((2, ROWS))],
+        compiler_params=pltpu.CompilerParams(vmem_limit_bytes=48 * 1024 * 1024),
+    )(came, jnp.take(bank, came_picks.reshape(-1), axis=0), fwd, inv, tw)
+    return jnp.take(result, (channel_order % n) * each + channel_order // n, axis=0)
+
+
+def local(raw_traces, filter_index, channel_order, wavelets, damping):
+    rows, length = raw_traces.shape
+    own, taps = wavelets.shape
+    n = lax.axis_size("traces")
+    if n % 2 or rows != n * ROWS or own % SUBLANES or own > LANES or taps % LANES:
+        return gathered(raw_traces, filter_index, channel_order, wavelets, damping)
+
+    fwd, inv, tw = tables(length, taps)
+    tiles = own // SUBLANES * (taps // LANES)
+    dma = pltpu.SemaphoreType.DMA
+    came = pl.pallas_call(
+        functools.partial(exchange_kernel, n, taps),
+        in_specs=[pl.BlockSpec(memory_space=pltpu.HBM)] * 7,
+        out_specs=pl.BlockSpec(memory_space=pltpu.VMEM),
+        out_shape=pltpu.VMEM((2 * n, ROWS, length), jnp.float32),
+        scratch_shapes=scratch()
+        + [pltpu.VMEM(a.shape, a.dtype) for a in (fwd, inv, tw)]
+        + [
+            pltpu.VMEM((n, tiles + 1, SUBLANES, LANES), jnp.float32),
+            pltpu.VMEM((ROWS, taps + LANES), jnp.float32),
+            pltpu.SMEM((2, rows), jnp.int32),
+            pltpu.SMEM((own,), jnp.float32),
+            dma((n,)),
+            dma((5 + tiles,)),
+            dma((2,)),
+            dma((2,)),
+            dma((n,)),
+            dma((n,)),
+            dma((n,)),
+            dma((n,)),
+        ],
+        compiler_params=pltpu.CompilerParams(
+            collective_id=0, has_side_effects=True, vmem_limit_bytes=40 * 1024 * 1024
         ),
+        cost_estimate=pl.CostEstimate(flops=rows * length * 1500, bytes_accessed=8 * rows * length, transcendentals=0),
+    )(raw_traces, filter_index, wavelets, damping, fwd, inv, tw)
+    came = pltpu.with_memory_space_constraint(came, pltpu.VMEM)
+    return pl.pallas_call(
+        functools.partial(settle_kernel, n),
+        in_specs=[pl.BlockSpec(memory_space=pltpu.SMEM), pl.BlockSpec(memory_space=pltpu.VMEM)],
+        out_specs=pl.BlockSpec(memory_space=pltpu.HBM),
         out_shape=jax.ShapeDtypeStruct((rows, length), jnp.float32),
-        compiler_params=params,
-        cost_estimate=flops,
-    )(row_of[:, 0].reshape(-1), came_raw, jnp.take(bank, came_rows, axis=0), fwd, inv, tw)
-    return pl.pallas_call(
-        settle_kernel,
-        in_specs=[pl.BlockSpec(memory_space=pltpu.SMEM)] + [pl.BlockSpec(memory_space=pl.ANY)] * 2,
-        out_specs=pl.BlockSpec(memory_space=pl.ANY),
-        out_shape=jax.ShapeDtypeStruct((rows, length), jnp.float32),
-        scratch_shapes=[
-            pltpu.VMEM((n, part, length), jnp.float32),
-            pltpu.SemaphoreType.DMA((n,)),
-            pltpu.SemaphoreType.DMA((n, part)),
-        ],
-        input_output_aliases={2: 0},
-        compiler_params=params,
-    )(row_of[:, 1].reshape(-1), came_done, filled)
+        scratch_shapes=[dma((n,))],
+        compiler_params=pltpu.CompilerParams(vmem_limit_bytes=20 * 1024 * 1024),
+    )(channel_order, came)
 
 
 def solution(mesh):

time: 231 us -> 192 us (0.83)
  Pallas kernels: 41.7 us -> 189 us
  waiting for transfers between devices: 144 us -> 0 us
  blocking collectives: 17.1 us -> 0 us
  starting transfers between devices: 15 us -> 0 us
  local copies, waits for them, and re-layouts: 9.22 us -> 0.01 us
  other arithmetic: 3.49 us -> 0 us
    pallas_call x3 -> x2, Pallas kernels: 41.7 us -> 189 us  [the longest x1 186 us: local(): pl.pallas_call(functools.partial(exchange_kernel, n, taps), in_specs=[pl....]
    all_to_all x2 -> x0, waiting for transfers between devices: 144 us -> none  [the longest x1 72.2 us: local(): came_raw = lax.all_to_all(first, 'traces', 0, 0, tiled=True)]
    all_gather x1 -> x0, blocking collectives: 17.1 us -> none  [local(): lax.all_gather(jnp.concatenate([wavelets, floor[:, None], picks], axis=1)...]
    all_to_all x2 -> x0, starting transfers between devices: 15 us -> none  [the longest x1 10.4 us: local(): came_raw = lax.all_to_all(first, 'traces', 0, 0, tiled=True)]
    slice x5 -> x0, local copies, waits for them, and re-layouts: 4.8 us -> none  [the longest x1 4.6 us: local(): first = raw_traces.reshape(n, each, length)[:, :part]]
  transfers between devices with their start and end apart: 2 -> 0, of which waited for: 2 -> 0; matrix products, arithmetic and copies ran while one was open for 1% -> 0% of each run, Pallas kernels for 16% -> 0%
where the time goes in v1:
time: 192 us; the launch traced here: 190 us
  Pallas kernels  189 us (98%)
    pallas_call x1, Pallas kernels, local(): pl.pallas_call(functools.partial(exchange_kernel, n, taps), in_specs=[pl....  186 us
    pallas_call x1, Pallas kernels, local(): pl.pallas_call(functools.partial(settle_kernel, n), in_specs=[pl.BlockSpe...  3.87 us

profile of v1, /device:TPU:16, one launch (start us, length us, event | category | flops | bytes accessed | tf_op | source)
XLA Modules:
  0.0 189.5 jit_solution(5481363938893687605)
XLA Ops:
  0.0 0.0 copy-start
  0.0 185.6 %shard_map.82.came_ref = f32[32,16,8192]{2,1,0:T(8,128)S(1)} custom-call(f32[256,8192]{1,0:T(8,128)} %x_ref.1, s32[256]{0:T(256)} %pick_ref.1, f32[16,256]{1,0:T(8,128)} %wave_ref.1, f32[16]{0:T(128)} %damp_ref.1, bf16[768,256]{1,0:T(8,128)(2,1)} %constant.6.clone.fwd_hbm, bf16[768,256]{1,0:T(8,128)(2,1)} %constant.7.clone.inv_hbm, ...), custom_call_target="tpu_custom_call" | custom-call | flops 3145728000 | bytes 16777216 | tf_op jit(solution)/shard_map/pallas_call | solution.py:523
  185.6 0.0 copy-done
  185.6 3.9 %shard_map.83 = f32[256,8192]{1,0:T(8,128)} custom-call(s32[256]{0:T(256)S(1)} %copy-done, f32[32,16,8192]{2,1,0:T(8,128)S(1)} %shard_map.82.came_ref), custom_call_target="tpu_custom_call" | custom-call | tf_op jit(solution)/shard_map/pallas_call | solution.py:550
Async XLA Ops:
  0.0 185.6 %copy-start = (s32[256]{0:T(256)S(1)}, s32[256]{0:T(256)}, u32[]{:S(2)}) copy-start(s32[256]{0:T(256)} %order_ref.1) | copy-start | bytes 3076

commit v2 on v1

--- a/solution.py
+++ b/solution.py
@@ -235,6 +235,16 @@
     while inner * inner < n:
         inner *= 2
     return (n // inner, inner) if n % inner == 0 else (1, n)
+
+
+def block_order(n):
+    inner = split_count(n)[1]
+    raws = [n - inner, (n - inner) ^ 1]
+    near = sorted(range(1, n // 2), key=lambda k: (k < inner, k))
+    cross = [k for k in range(n // 2, n) if k not in raws]
+    lead, rest = cross[:inner], cross[inner:]
+    mixed = lead[:1] + [k for pair in zip(lead[1:], near) for k in pair]
+    return mixed + near[max(len(lead) - 1, 0) :] + rest + raws + [0], raws
 
 
 def exchange_kernel(
@@ -264,14 +274,14 @@
     pick_sems,
     bank_sends,
     bank_recvs,
+    ready_sems,
     sends,
     recvs,
 ):
     me = lax.axis_index("traces")
     own, each = wave_ref.shape[0], x_ref.shape[0] // n
-    half = n // 2
-    partner = lax.rem(me + half, n)
     outer, inner = split_count(n)
+    partner = me ^ (n - inner)
     far, near = lax.div(me, inner), lax.rem(me, inner)
     halves, pieces = own // SUBLANES, taps // LANES
     last = halves * pieces
@@ -289,17 +299,42 @@
     def block_of(e):
         return x_ref.at[pl.ds(pl.multiple_of(e * each, each), each)]
 
+    turns, raws = block_order(n)
+    made = n - 1 - len(raws)
+
+    def turn_of(s):
+        k = 0
+        for i, turn in enumerate(turns):
+            k = jnp.where(s == i, turn, k)
+        return k
+
     barrier = pltpu.get_barrier_semaphore()
 
-    def greet(k, carry):
-        other = lax.rem(me + k, n)
-        pl.semaphore_signal(barrier, inc=1, device_id={"traces": other}, device_id_type=pl.DeviceIdType.MESH)
-        return carry
-
-    lax.fori_loop(1, n, greet, 0)
+    def tell(sem, other):
+        pl.semaphore_signal(sem, inc=1, device_id={"traces": other}, device_id_type=pl.DeviceIdType.MESH)
+
+    def greet(other, carry):
+        tell(barrier, other)
+        return carry
+
+    def answer(other, carry):
+        @pl.when(other != partner)
+        def _():
+            tell(ready_sems.at[me], other)
+
+        return carry
+
+    def meet(other, carry):
+        @pl.when(other != partner)
+        def _():
+            pl.semaphore_wait(ready_sems.at[other], 1)
+
+        return carry
+
+    lax.fori_loop(me + 1, n, greet, 0)
 
     damp_in = pltpu.make_async_copy(damp_ref, damp_smem, near_sems.at[0])
-    pick_in = pltpu.make_async_copy(pick_ref, pick_smem.at[0], near_sems.at[1])
+    pick_in = pltpu.make_async_copy(pick_ref, pick_smem.at[pl.ds(0, n * each)], near_sems.at[1])
     tables_in = [
         pltpu.make_async_copy(there, here, near_sems.at[2 + i])
         for i, (there, here) in enumerate(((fwd_hbm, fwd_ref), (inv_hbm, inv_ref), (tw_hbm, tw_ref)))
@@ -319,83 +354,133 @@
     def load(e):
         return pltpu.make_async_copy(block_of(e), buf_ref.at[n + e], load_sems.at[e])
 
-    def load_start(k, carry):
-        @pl.when(k != half)
+    def load_start(s, carry):
+        @pl.when(jnp.logical_or(s < made, s == n - 1))
         def _():
-            load(lax.rem(me + k, n)).start()
-
-        return carry
-
-    lax.fori_loop(1, n + 1, load_start, 0)
-
+            load(me ^ turn_of(s)).start()
+
+        return carry
+
+    def raw(i, part, here):
+        first, count, other = part * (each // 2), each // 2, me ^ raws[i]
+        rows = x_ref.at[pl.ds(pl.multiple_of(other * each + first, count), count)]
+        there = buf_ref.at[n + jnp.where(here, other, me), pl.ds(first, count)]
+        return remote(rows, there, raw_sems.at[0, i, part], raw_sems.at[1, i, part], other)
+
+    def picks(i):
+        count = n * each
+        there = pick_smem.at[pl.ds((1 + i) * count, count)]
+        return remote(pick_ref, there, pick_sems.at[0, i], pick_sems.at[1, i], me ^ raws[i])
+
+    @pl.when(me > 0)
+    def _():
+        pl.semaphore_wait(barrier, me)
+
+    @pl.when(partner < me)
+    def _():
+        tell(ready_sems.at[me], partner)
+
+    @pl.when(partner > me)
+    def _():
+        pl.semaphore_wait(ready_sems.at[partner], 1)
+
+    raw(0, 0, False).start()
+    lax.fori_loop(0, me, answer, 0)
     damp_in.wait()
     lane = lax.broadcasted_iota(jnp.int32, (SUBLANES, LANES), 1)
     levels = jnp.zeros((SUBLANES, LANES), jnp.float32)
     for f in range(own):
         levels = jnp.where(lane == f, damp_smem[f], levels)
     bank_ref[me, last] = levels
+    lax.fori_loop(me + 1, n, meet, 0)
     for copy in tiles_in:
         copy.wait()
-    pl.semaphore_wait(barrier, n - 1)
-
-    def far_copy(t):
-        there = lax.rem(far + t, outer) * inner + near
-        return remote(bank_ref.at[me], bank_ref.at[me], bank_sends.at[t - 1], bank_recvs.at[me], there)
-
-    def near_copy(t, d):
-        block = lax.rem(far + t, outer) * inner + near
-        there = far * inner + lax.rem(near + d, inner)
-        slot = outer - 1 + (d - 1) * outer + t
+
+    def bank_copy(block, slot, there):
         return remote(bank_ref.at[block], bank_ref.at[block], bank_sends.at[slot], bank_recvs.at[block], there)
 
+    def block_at(f):
+        return f * inner + near
+
+    middle = outer // 2
+    upper = far >= middle
+    gate = jnp.where(upper, middle, middle - 1)
+
+    def across(t, act):
+        there = lax.rem(far + t, outer)
+        direct = jnp.logical_or((there >= middle) == upper, there == outer - 1 - gate)
+
+        @pl.when(direct)
+        def _():
+            act(bank_copy(me, t - 1, block_at(there)))
+
+    def onward(t, act):
+        block = lax.rem(far + t, outer)
+        for there in range(outer):
+            slot = outer - 1 + (t - 1) * outer + there
+            near_side = (there >= middle) == upper
+            foreign = (block >= middle) != upper
+            go = jnp.logical_and(jnp.logical_and(far == gate, far != there), jnp.logical_and(near_side, foreign))
+
+            @pl.when(go)
+            def _():
+                act(bank_copy(block_at(block), slot, block_at(there)))
+
+    def spread(f, act):
+        for d in range(1, inner):
+            slot = outer * outer - 1 + f * (inner - 1) + d - 1
+            act(bank_copy(block_at(f), slot, far * inner + (near ^ d)))
+
     def bank_came(block):
-        return remote(bank_ref.at[block], bank_ref.at[block], bank_sends.at[0], bank_recvs.at[block], partner)
-
+        bank_copy(block, 0, partner).wait_recv()
+
+    start, sent = (lambda copy: copy.start()), (lambda copy: copy.wait_send())
     for t in range(1, outer):
-        far_copy(t).start()
-    raw_out = remote(block_of(partner), buf_ref.at[n + me], raw_sems.at[0], raw_sems.at[1], partner)
-    raw_came = remote(block_of(partner), buf_ref.at[n + partner], raw_sems.at[0], raw_sems.at[1], partner)
-    picks_out = remote(pick_ref, pick_smem.at[1], pick_sems.at[0], pick_sems.at[1], partner)
-    raw_out.start()
-    picks_out.start()
-    for d in range(1, inner):
-        near_copy(0, d).start()
+        across(t, start)
+    spread(far, start)
+    raw(0, 1, False).start()
+    for i in range(1, len(raws)):
+        raw(i, 0, False).start()
+        raw(i, 1, False).start()
+    for i in range(len(raws)):
+        picks(i).start()
+    lax.fori_loop(0, n, load_start, 0)
     for t in range(1, outer):
-        bank_came(lax.rem(far + t, outer) * inner + near).wait_recv()
+        block = lax.rem(far + t, outer)
+        bank_came(block_at(block))
+        onward(t, start)
+        spread(block, start)
+    for f in range(outer):
         for d in range(1, inner):
-            near_copy(t, d).start()
-    for d in range(1, inner):
-        for t in range(outer):
-            bank_came(lax.rem(far + t, outer) * inner + lax.rem(near + d, inner)).wait_recv()
+            bank_came(f * inner + (near ^ d))
     pick_in.wait()
     for copy in tables_in:
         copy.wait()
 
-    def turn_of(s):
-        return jnp.where(s < half - 1, s + 1, jnp.where(s < n - 2, s + 2, jnp.where(s == n - 2, half, 0)))
-
     def send(e):
         return remote(buf_ref.at[n + e], buf_ref.at[me], sends.at[e], recvs.at[me], e)
 
     row_lane = lax.broadcasted_iota(jnp.int32, (1, LANES), 1)
 
     def step(s, carry):
-        e = lax.rem(me + turn_of(s), n)
-        theirs = s == n - 2
-
-        @pl.when(theirs)
-        def _():
-            raw_came.wait_recv()
-            picks_out.wait_recv()
+        e = me ^ turn_of(s)
+        theirs = jnp.logical_and(s >= made, s < n - 1)
+        for i in range(len(raws)):
+
+            @pl.when(s == made + i)
+            def _():
+                raw(i, 0, True).wait_recv()
+                raw(i, 1, True).wait_recv()
+                picks(i).wait_recv()
 
         @pl.when(jnp.logical_not(theirs))
         def _():
             load(e).wait()
 
-        table = jnp.where(theirs, 1, 0)
-        base = jnp.where(theirs, me, e) * each
+        table = jnp.where(theirs, s - made + 1, 0)
+        base = (table * n + jnp.where(theirs, me, e)) * each
         for r in range(ROWS):
-            pick = pick_smem[table, base + r]
+            pick = pick_smem[base + r]
             block, inside = lax.div(pick, own), lax.rem(pick, own)
             tile, sub = lax.div(inside, SUBLANES) * pieces, lax.rem(inside, SUBLANES)
             for p in range(pieces):
@@ -403,11 +488,11 @@
             level = bank_ref[block, last, 0:1, :]
             rows_ref[r : r + 1, taps : taps + LANES] = jnp.where(row_lane == inside, level, 0.0)
 
-        @pl.when(jnp.logical_and(s >= 1, s <= n - 2))
+        @pl.when(jnp.logical_and(s >= 1, s <= made))
         def _():
-            send(lax.rem(me + turn_of(s - 1), n)).start()
-
-        slot = jnp.where(s >= n - 2, e, n + e)
+            send(me ^ turn_of(s - 1)).start()
+
+        slot = jnp.where(s >= made, e, n + e)
         wave = [rows_ref[:, p * LANES : (p + 1) * LANES] for p in range(pieces)]
         power = sum(jnp.sum(w * w, axis=1, keepdims=True) for w in wave)
         damp = jnp.sum(rows_ref[:, taps : taps + LANES], axis=1, keepdims=True)
@@ -424,35 +509,34 @@
 
     lax.fori_loop(0, n, step, 0)
 
-    raw_out.wait_send()
-    picks_out.wait_send()
+    for i in range(len(raws)):
+        raw(i, 0, False).wait_send()
+        raw(i, 1, False).wait_send()
+        picks(i).wait_send()
     for t in range(1, outer):
-        far_copy(t).wait_send()
-    for d in range(1, inner):
-        for t in range(outer):
-            near_copy(t, d).wait_send()
-
-    def finish(k, carry):
-        @pl.when(k != half)
-        def _():
-            e = lax.rem(me + k, n)
-            send(e).wait_send()
-            remote(buf_ref.at[e], buf_ref.at[e], sends.at[e], recvs.at[e], e).wait_recv()
-
-        return carry
-
-    lax.fori_loop(1, n, finish, 0)
+        across(t, sent)
+        onward(t, sent)
+    for f in range(outer):
+        spread(f, sent)
+
+    def finish(s, carry):
+        e = me ^ turn_of(s)
+        send(e).wait_send()
+        remote(buf_ref.at[e], buf_ref.at[e], sends.at[e], recvs.at[e], e).wait_recv()
+        return carry
+
+    lax.fori_loop(0, made, finish, 0)
 
 
 def settle_kernel(n, order_ref, came_ref, o_ref, sems):
-    rows = o_ref.shape[0]
-    each = rows // n
+    each = o_ref.shape[0] // n
+    shift = n.bit_length() - 1
 
     def put(d, carry):
         for r in range(each):
             q = d * each + r
             place = order_ref[q]
-            came = came_ref.at[lax.rem(place, n), pl.ds(lax.div(place, n), 1)]
+            came = came_ref.at[place & (n - 1), pl.ds(place >> shift, 1)]
             pltpu.make_async_copy(came, o_ref.at[pl.ds(q, 1)], sems.at[d]).start()
         return carry
 
@@ -514,11 +598,13 @@
     rows, length = raw_traces.shape
     own, taps = wavelets.shape
     n = lax.axis_size("traces")
-    if n % 2 or rows != n * ROWS or own % SUBLANES or own > LANES or taps % LANES:
+    if n < 4 or n & (n - 1) or rows != n * ROWS or own % SUBLANES or own > LANES or taps % LANES:
         return gathered(raw_traces, filter_index, channel_order, wavelets, damping)
 
     fwd, inv, tw = tables(length, taps)
     tiles = own // SUBLANES * (taps // LANES)
+    outer = split_count(n)[0]
+    raws = len(block_order(n)[1])
     dma = pltpu.SemaphoreType.DMA
     came = pl.pallas_call(
         functools.partial(exchange_kernel, n, taps),
@@ -530,14 +616,15 @@
         + [
             pltpu.VMEM((n, tiles + 1, SUBLANES, LANES), jnp.float32),
             pltpu.VMEM((ROWS, taps + LANES), jnp.float32),
-            pltpu.SMEM((2, rows), jnp.int32),
+            pltpu.SMEM(((1 + raws) * rows,), jnp.int32),
             pltpu.SMEM((own,), jnp.float32),
             dma((n,)),
             dma((5 + tiles,)),
-            dma((2,)),
-            dma((2,)),
+            dma((2, raws, 2)),
+            dma((2, raws)),
+            dma((outer * outer - 1 + n - outer,)),
             dma((n,)),
-            dma((n,)),
+            pltpu.SemaphoreType.REGULAR((n,)),
             dma((n,)),
             dma((n,)),
         ],

time: 192 us -> 190 us (0.990)
  no operation moved by 1% of the time
where the time goes in v2:
time: 190 us; the launch traced here: 189 us
  Pallas kernels  189 us (99%)
    pallas_call x1, Pallas kernels, local(): pl.pallas_call(functools.partial(exchange_kernel, n, taps), in_specs=[pl....  185 us
    pallas_call x1, Pallas kernels, local(): pl.pallas_call(functools.partial(settle_kernel, n), in_specs=[pl.BlockSpe...  3.87 us

profile of v2, /device:TPU:16, one launch (start us, length us, event | category | flops | bytes accessed | tf_op | source)
XLA Modules:
  0.0 189.4 jit_solution(9283596689989857769)
XLA Ops:
  0.0 0.0 copy-start
  0.0 185.5 %shard_map.82.came_ref = f32[32,16,8192]{2,1,0:T(8,128)S(1)} custom-call(f32[256,8192]{1,0:T(8,128)} %x_ref.1, s32[256]{0:T(256)} %pick_ref.1, f32[16,256]{1,0:T(8,128)} %wave_ref.1, f32[16]{0:T(128)} %damp_ref.1, bf16[768,256]{1,0:T(8,128)(2,1)} %constant.6.clone.fwd_hbm, bf16[768,256]{1,0:T(8,128)(2,1)} %constant.7.clone.inv_hbm, ...), custom_call_target="tpu_custom_call" | custom-call | flops 3145728000 | bytes 16777216 | tf_op jit(solution)/shard_map/pallas_call | solution.py:609
  185.5 0.0 copy-done
  185.5 3.9 %shard_map.83 = f32[256,8192]{1,0:T(8,128)} custom-call(s32[256]{0:T(256)S(1)} %copy-done, f32[32,16,8192]{2,1,0:T(8,128)S(1)} %shard_map.82.came_ref), custom_call_target="tpu_custom_call" | custom-call | tf_op jit(solution)/shard_map/pallas_call | solution.py:637
Async XLA Ops:
  0.0 185.5 %copy-start = (s32[256]{0:T(256)S(1)}, s32[256]{0:T(256)}, u32[]{:S(2)}) copy-start(s32[256]{0:T(256)} %order_ref.1) | copy-start | bytes 3076

commit v3 on v2

--- a/solution.py
+++ b/solution.py
@@ -239,12 +239,19 @@
 
 def block_order(n):
     inner = split_count(n)[1]
-    raws = [n - inner, (n - inner) ^ 1]
+    raws = list(range(n - inner + 1, n, 2))[:2]
+    kept = list(range(n - inner, n, 2))[:2]
     near = sorted(range(1, n // 2), key=lambda k: (k < inner, k))
-    cross = [k for k in range(n // 2, n) if k not in raws]
+    cross = [k for k in range(n // 2, n) if k not in raws + kept]
     lead, rest = cross[:inner], cross[inner:]
     mixed = lead[:1] + [k for pair in zip(lead[1:], near) for k in pair]
-    return mixed + near[max(len(lead) - 1, 0) :] + rest + raws + [0], raws
+    return mixed + near[max(len(lead) - 1, 0) :] + rest + kept + raws + [0], raws, kept
+
+
+def keeps_blocks(me, n):
+    outer, inner = split_count(n)
+    far = lax.div(me, inner)
+    return jnp.logical_and(me % 2 == 0, jnp.logical_or(far == outer // 2 - 1, far == outer // 2))
 
 
 def exchange_kernel(
@@ -281,7 +288,6 @@
     me = lax.axis_index("traces")
     own, each = wave_ref.shape[0], x_ref.shape[0] // n
     outer, inner = split_count(n)
-    partner = me ^ (n - inner)
     far, near = lax.div(me, inner), lax.rem(me, inner)
     halves, pieces = own // SUBLANES, taps // LANES
     last = halves * pieces
@@ -299,8 +305,10 @@
     def block_of(e):
         return x_ref.at[pl.ds(pl.multiple_of(e * each, each), each)]
 
-    turns, raws = block_order(n)
+    turns, raws, kept = block_order(n)
+    partner = me ^ raws[0]
     made = n - 1 - len(raws)
+    sent_here = made - jnp.where(keeps_blocks(me, n), len(kept), 0)
 
     def turn_of(s):
         k = 0
@@ -488,7 +496,7 @@
             level = bank_ref[block, last, 0:1, :]
             rows_ref[r : r + 1, taps : taps + LANES] = jnp.where(row_lane == inside, level, 0.0)
 
-        @pl.when(jnp.logical_and(s >= 1, s <= made))
+        @pl.when(jnp.logical_and(s >= 1, s <= sent_here))
         def _():
             send(me ^ turn_of(s - 1)).start()
 
@@ -525,29 +533,90 @@
         remote(buf_ref.at[e], buf_ref.at[e], sends.at[e], recvs.at[e], e).wait_recv()
         return carry
 
-    lax.fori_loop(0, made, finish, 0)
-
-
-def settle_kernel(n, order_ref, came_ref, o_ref, sems):
-    each = o_ref.shape[0] // n
+    lax.fori_loop(0, sent_here, finish, 0)
+
+
+def late_kernel(n, buf_ref, after_ref, late_ref, sends, recvs):
+    del after_ref
+    me = lax.axis_index("traces")
+    kept = block_order(n)[2]
+
+    @pl.when(keeps_blocks(me, n))
+    def _():
+        barrier = pltpu.get_barrier_semaphore()
+        for k in kept:
+            pl.semaphore_signal(barrier, inc=1, device_id={"traces": me ^ k}, device_id_type=pl.DeviceIdType.MESH)
+        pl.semaphore_wait(barrier, len(kept))
+        copies = [
+            pltpu.make_async_remote_copy(
+                src_ref=buf_ref.at[n + (me ^ k)],
+                dst_ref=late_ref.at[i],
+                send_sem=sends.at[i],
+                recv_sem=recvs.at[i],
+                device_id={"traces": me ^ k},
+                device_id_type=pl.DeviceIdType.MESH,
+            )
+            for i, k in enumerate(kept)
+        ]
+        for copy in copies:
+            copy.start()
+        for copy in copies:
+            copy.wait()
+
+
+def settle_kernel(n, order_ref, came_ref, o_ref, late_rows_ref, sem):
+    rows = o_ref.shape[0]
+    each = rows // n
     shift = n.bit_length() - 1
+    me = lax.axis_index("traces")
+    kept = block_order(n)[2]
+    keeps = keeps_blocks(me, n)
 
     def put(d, carry):
         for r in range(each):
             q = d * each + r
             place = order_ref[q]
-            came = came_ref.at[place & (n - 1), pl.ds(place >> shift, 1)]
-            pltpu.make_async_copy(came, o_ref.at[pl.ds(q, 1)], sems.at[d]).start()
+            source, row = place & (n - 1), place >> shift
+            turn = source ^ me
+            late = jnp.logical_and(keeps, functools.reduce(jnp.logical_or, [turn == k for k in kept]))
+
+            @pl.when(late)
+            def _():
+                index = functools.reduce(lambda at, ik: jnp.where(turn == ik[1], ik[0], at), enumerate(kept), 0)
+                late_rows_ref[index * each + row] = q
+
+            @pl.when(jnp.logical_not(late))
+            def _():
+                pltpu.make_async_copy(came_ref.at[source, pl.ds(row, 1)], o_ref.at[pl.ds(q, 1)], sem).start()
+
         return carry
 
     lax.fori_loop(0, n, put, 0)
 
-    def finish(d, carry):
-        part = o_ref.at[pl.ds(pl.multiple_of(d * each, each), each)]
-        pltpu.make_async_copy(came_ref.at[0], part, sems.at[d]).wait()
-        return carry
-
-    lax.fori_loop(0, n, finish, 0)
+    def finish(count):
+        pltpu.make_async_copy(o_ref.at[pl.ds(0, count)], o_ref.at[pl.ds(0, count)], sem).wait()
+
+    @pl.when(keeps)
+    def _():
+        finish(rows - len(kept) * each)
+
+    @pl.when(jnp.logical_not(keeps))
+    def _():
+        finish(rows)
+
+
+def last_kernel(n, late_rows_ref, late_ref, settled_ref, o_ref, sem):
+    del settled_ref
+    count, each, _ = late_ref.shape
+
+    @pl.when(keeps_blocks(lax.axis_index("traces"), n))
+    def _():
+        for i in range(count):
+            for r in range(each):
+                q = late_rows_ref[i * each + r]
+                pltpu.make_async_copy(late_ref.at[i, pl.ds(r, 1)], o_ref.at[pl.ds(q, 1)], sem).start()
+        part = o_ref.at[pl.ds(0, count * each)]
+        pltpu.make_async_copy(part, part, sem).wait()
 
 
 def tables(length, taps):
@@ -604,7 +673,8 @@
     fwd, inv, tw = tables(length, taps)
     tiles = own // SUBLANES * (taps // LANES)
     outer = split_count(n)[0]
-    raws = len(block_order(n)[1])
+    _, raws, kept = block_order(n)
+    raws, kept = len(raws), len(kept)
     dma = pltpu.SemaphoreType.DMA
     came = pl.pallas_call(
         functools.partial(exchange_kernel, n, taps),
@@ -634,14 +704,39 @@
         cost_estimate=pl.CostEstimate(flops=rows * length * 1500, bytes_accessed=8 * rows * length, transcendentals=0),
     )(raw_traces, filter_index, wavelets, damping, fwd, inv, tw)
     came = pltpu.with_memory_space_constraint(came, pltpu.VMEM)
+    smem, vmem, hbm = (pl.BlockSpec(memory_space=m) for m in (pltpu.SMEM, pltpu.VMEM, pltpu.HBM))
+    params = pltpu.CompilerParams(vmem_limit_bytes=20 * 1024 * 1024)
+    settled, late_rows = pl.pallas_call(
+        functools.partial(settle_kernel, n),
+        in_specs=[smem, vmem],
+        out_specs=[hbm, smem],
+        out_shape=[
+            jax.ShapeDtypeStruct((rows, length), jnp.float32),
+            jax.ShapeDtypeStruct((kept * ROWS,), jnp.int32),
+        ],
+        scratch_shapes=[dma],
+        compiler_params=params,
+    )(channel_order, came)
+    late = pl.pallas_call(
+        functools.partial(late_kernel, n),
+        in_specs=[vmem, pl.BlockSpec(memory_space=pl.ANY)],
+        out_specs=vmem,
+        out_shape=pltpu.VMEM((kept, ROWS, length), jnp.float32),
+        scratch_shapes=[dma((kept,)), dma((kept,))],
+        compiler_params=pltpu.CompilerParams(
+            collective_id=1, has_side_effects=True, vmem_limit_bytes=20 * 1024 * 1024
+        ),
+    )(came, late_rows)
+    late = pltpu.with_memory_space_constraint(late, pltpu.VMEM)
     return pl.pallas_call(
-        functools.partial(settle_kernel, n),
-        in_specs=[pl.BlockSpec(memory_space=pltpu.SMEM), pl.BlockSpec(memory_space=pltpu.VMEM)],
-        out_specs=pl.BlockSpec(memory_space=pltpu.HBM),
+        functools.partial(last_kernel, n),
+        in_specs=[smem, vmem, hbm],
+        out_specs=hbm,
         out_shape=jax.ShapeDtypeStruct((rows, length), jnp.float32),
-        scratch_shapes=[dma((n,))],
-        compiler_params=pltpu.CompilerParams(vmem_limit_bytes=20 * 1024 * 1024),
-    )(channel_order, came)
+        scratch_shapes=[dma],
+        input_output_aliases={2: 0},
+        compiler_params=params,
+    )(late_rows, late, settled)
 
 
 def solution(mesh):

time: 190 us -> 187 us (0.984)
  Pallas kernels: 189 us -> 187 us
    pallas_call x1, Pallas kernels: 185 us -> 162 us  [local(): pl.pallas_call(functools.partial(exchange_kernel, n, taps), in_specs=[pl....]
    pallas_call x1 -> x3, Pallas kernels: 3.87 us -> 24.8 us  [the longest x1 19.1 us: local(): pl.pallas_call(functools.partial(late_kernel, n), in_specs=[vmem, pl.Bloc...]
where the time goes in v3:
time: 187 us
  Pallas kernels  187 us (100%)
    pallas_call x1, Pallas kernels, local(): pl.pallas_call(functools.partial(exchange_kernel, n, taps), in_specs=[pl....  162 us
    pallas_call x1, Pallas kernels, local(): pl.pallas_call(functools.partial(late_kernel, n), in_specs=[vmem, pl.Bloc...  19.1 us
    pallas_call x1, Pallas kernels, local(): pl.pallas_call(functools.partial(settle_kernel, n), in_specs=[smem, vmem]...  4.14 us

profile of v3, /device:TPU:16, one launch (start us, length us, event | category | flops | bytes accessed | tf_op | source)
XLA Modules:
  0.0 187.1 jit_solution(17604102135343542447)
XLA Ops:
  0.0 0.0 copy-start
  0.0 162.3 %shard_map.82.came_ref.buf_ref = f32[32,16,8192]{2,1,0:T(8,128)S(1)} custom-call(f32[256,8192]{1,0:T(8,128)} %x_ref.1, s32[256]{0:T(256)} %pick_ref.1, f32[16,256]{1,0:T(8,128)} %wave_ref.1, f32[16]{0:T(128)} %damp_ref.1, bf16[768,256]{1,0:T(8,128)(2,1)} %constant.6.clone.fwd_hbm, bf16[768,256]{1,0:T(8,128)(2,1)} %constant.7.clone.inv_hbm, ...), custom_call_target="tpu_custom_call" | custom-call | flops 3145728000 | bytes 16777216 | tf_op jit(solution)/shard_map/pallas_call | solution.py:679
  162.3 0.0 copy-done
  162.3 4.1 %shard_map.83 = (f32[256,8192]{1,0:T(8,128)}, s32[32]{0:T(128)S(1)}) custom-call(s32[256]{0:T(256)S(1)} %copy-done, f32[32,16,8192]{2,1,0:T(8,128)S(1)} %shard_map.82.came_ref.buf_ref), custom_call_target="tpu_custom_call" | custom-call | tf_op jit(solution)/shard_map/pallas_call | solution.py:709
  166.4 19.1 %shard_map.84.late_ref = f32[2,16,8192]{2,1,0:T(8,128)S(1)} custom-call(f32[32,16,8192]{2,1,0:T(8,128)S(1)} %shard_map.82.came_ref.buf_ref, s32[32]{0:T(128)S(1)} %get-tuple-element.7.after_ref.late_rows_ref), custom_call_target="tpu_custom_call" | custom-call | tf_op jit(solution)/shard_map/pallas_call | solution.py:720
  185.6 1.5 shard_map.85
Async XLA Ops:
  0.0 162.3 %copy-start = (s32[256]{0:T(256)S(1)}, s32[256]{0:T(256)}, u32[]{:S(2)}) copy-start(s32[256]{0:T(256)} %order_ref.1) | copy-start | bytes 3076

commit v4 on v3

--- a/solution.py
+++ b/solution.py
@@ -240,7 +240,7 @@
 def block_order(n):
     inner = split_count(n)[1]
     raws = list(range(n - inner + 1, n, 2))[:2]
-    kept = list(range(n - inner, n, 2))[:2]
+    kept = list(range(n - inner, n, 2))[1::-1]
     near = sorted(range(1, n // 2), key=lambda k: (k < inner, k))
     cross = [k for k in range(n // 2, n) if k not in raws + kept]
     lead, rest = cross[:inner], cross[inner:]
@@ -273,8 +273,10 @@
     tw_ref,
     bank_ref,
     rows_ref,
+    stage_ref,
     pick_smem,
     damp_smem,
+    stage_sem,
     load_sems,
     near_sems,
     raw_sems,
@@ -339,7 +341,33 @@
 
         return carry
 
+    def raw(i, part, here):
+        first, count, other = part * (each // 2), each // 2, me ^ raws[i]
+        rows = x_ref.at[pl.ds(pl.multiple_of(other * each + first, count), count)]
+        there = buf_ref.at[n + jnp.where(here, other, me), pl.ds(first, count)]
+        return remote(rows, there, raw_sems.at[0, i, part], raw_sems.at[1, i, part], other)
+
+    def raw_staged():
+        there = buf_ref.at[n + me, pl.ds(0, each // 2)]
+        return remote(stage_ref, there, raw_sems.at[0, 0, 0], raw_sems.at[1, 0, 0], partner)
+
+    stage = pl.ds(pl.multiple_of(partner * each, each // 2), each // 2)
+    stage_in = pltpu.make_async_copy(x_ref.at[stage], stage_ref, stage_sem)
+
+    @pl.when(partner > me)
+    def _():
+        stage_in.start()
+
     lax.fori_loop(me + 1, n, greet, 0)
+
+    @pl.when(me > 0)
+    def _():
+        pl.semaphore_wait(barrier, me)
+
+    @pl.when(partner < me)
+    def _():
+        tell(ready_sems.at[me], partner)
+        raw(0, 0, False).start()
 
     damp_in = pltpu.make_async_copy(damp_ref, damp_smem, near_sems.at[0])
     pick_in = pltpu.make_async_copy(pick_ref, pick_smem.at[pl.ds(0, n * each)], near_sems.at[1])
@@ -369,30 +397,17 @@
 
         return carry
 
-    def raw(i, part, here):
-        first, count, other = part * (each // 2), each // 2, me ^ raws[i]
-        rows = x_ref.at[pl.ds(pl.multiple_of(other * each + first, count), count)]
-        there = buf_ref.at[n + jnp.where(here, other, me), pl.ds(first, count)]
-        return remote(rows, there, raw_sems.at[0, i, part], raw_sems.at[1, i, part], other)
-
     def picks(i):
         count = n * each
         there = pick_smem.at[pl.ds((1 + i) * count, count)]
         return remote(pick_ref, there, pick_sems.at[0, i], pick_sems.at[1, i], me ^ raws[i])
 
-    @pl.when(me > 0)
-    def _():
-        pl.semaphore_wait(barrier, me)
-
-    @pl.when(partner < me)
-    def _():
-        tell(ready_sems.at[me], partner)
-
     @pl.when(partner > me)
     def _():
+        stage_in.wait()
         pl.semaphore_wait(ready_sems.at[partner], 1)
-
-    raw(0, 0, False).start()
+        raw_staged().start()
+
     lax.fori_loop(0, me, answer, 0)
     damp_in.wait()
     lane = lax.broadcasted_iota(jnp.int32, (SUBLANES, LANES), 1)
@@ -686,8 +701,10 @@
         + [
             pltpu.VMEM((n, tiles + 1, SUBLANES, LANES), jnp.float32),
             pltpu.VMEM((ROWS, taps + LANES), jnp.float32),
+            pltpu.VMEM((ROWS // 2, length), jnp.float32),
             pltpu.SMEM(((1 + raws) * rows,), jnp.int32),
             pltpu.SMEM((own,), jnp.float32),
+            dma,
             dma((n,)),
             dma((5 + tiles,)),
             dma((2, raws, 2)),

time: 187 us -> 187 us (level)
  no operation moved by 1% of the time
where the time goes in v4:
time: 187 us
  Pallas kernels  187 us (100%)
    pallas_call x1, Pallas kernels, local(): pl.pallas_call(functools.partial(exchange_kernel, n, taps), in_specs=[pl....  162 us
    pallas_call x1, Pallas kernels, local(): pl.pallas_call(functools.partial(late_kernel, n), in_specs=[vmem, pl.Bloc...  18.9 us
    pallas_call x1, Pallas kernels, local(): pl.pallas_call(functools.partial(settle_kernel, n), in_specs=[smem, vmem]...  4.15 us

profile of v4, /device:TPU:16, one launch (start us, length us, event | category | flops | bytes accessed | tf_op | source)
XLA Modules:
  0.0 186.8 jit_solution(9998101961447529636)
XLA Ops:
  0.0 0.0 copy-start
  0.0 162.3 %shard_map.82.came_ref.buf_ref = f32[32,16,8192]{2,1,0:T(8,128)S(1)} custom-call(f32[256,8192]{1,0:T(8,128)} %x_ref.1, s32[256]{0:T(256)} %pick_ref.1, f32[16,256]{1,0:T(8,128)} %wave_ref.1, f32[16]{0:T(128)} %damp_ref.1, bf16[768,256]{1,0:T(8,128)(2,1)} %constant.6.clone.fwd_hbm, bf16[768,256]{1,0:T(8,128)(2,1)} %constant.7.clone.inv_hbm, ...), custom_call_target="tpu_custom_call" | custom-call | flops 3145728000 | bytes 16777216 | tf_op jit(solution)/shard_map/pallas_call | solution.py:694
  162.3 0.0 copy-done
  162.3 4.1 %shard_map.83 = (f32[256,8192]{1,0:T(8,128)}, s32[32]{0:T(128)S(1)}) custom-call(s32[256]{0:T(256)S(1)} %copy-done, f32[32,16,8192]{2,1,0:T(8,128)S(1)} %shard_map.82.came_ref.buf_ref), custom_call_target="tpu_custom_call" | custom-call | tf_op jit(solution)/shard_map/pallas_call | solution.py:726
  166.4 18.9 %shard_map.84.late_ref = f32[2,16,8192]{2,1,0:T(8,128)S(1)} custom-call(f32[32,16,8192]{2,1,0:T(8,128)S(1)} %shard_map.82.came_ref.buf_ref, s32[32]{0:T(128)S(1)} %get-tuple-element.7.after_ref.late_rows_ref), custom_call_target="tpu_custom_call" | custom-call | tf_op jit(solution)/shard_map/pallas_call | solution.py:737
  185.3 1.5 shard_map.85
Async XLA Ops:
  0.0 162.3 %copy-start = (s32[256]{0:T(256)S(1)}, s32[256]{0:T(256)}, u32[]{:S(2)}) copy-start(s32[256]{0:T(256)} %order_ref.1) | copy-start | bytes 3076

commit v5 on v4

--- a/solution.py
+++ b/solution.py
@@ -378,7 +378,7 @@
     tiles_in = [
         pltpu.make_async_copy(
             wave_ref.at[pl.ds(h * SUBLANES, SUBLANES), pl.ds(p * LANES, LANES)],
-            bank_ref.at[me, h * pieces + p],
+            bank_ref.at[me, pl.ds((h * pieces + p) * SUBLANES, SUBLANES)],
             near_sems.at[5 + h * pieces + p],
         )
         for h in range(halves)
@@ -414,13 +414,14 @@
     levels = jnp.zeros((SUBLANES, LANES), jnp.float32)
     for f in range(own):
         levels = jnp.where(lane == f, damp_smem[f], levels)
-    bank_ref[me, last] = levels
+    bank_ref[me, last * SUBLANES : (last + 1) * SUBLANES, :] = levels
     lax.fori_loop(me + 1, n, meet, 0)
     for copy in tiles_in:
         copy.wait()
 
     def bank_copy(block, slot, there):
-        return remote(bank_ref.at[block], bank_ref.at[block], bank_sends.at[slot], bank_recvs.at[block], there)
+        used = bank_ref.at[block, pl.ds(0, last * SUBLANES + 1)]
+        return remote(used, used, bank_sends.at[slot], bank_recvs.at[block], there)
 
     def block_at(f):
         return f * inner + near
@@ -505,10 +506,10 @@
         for r in range(ROWS):
             pick = pick_smem[base + r]
             block, inside = lax.div(pick, own), lax.rem(pick, own)
-            tile, sub = lax.div(inside, SUBLANES) * pieces, lax.rem(inside, SUBLANES)
+            at = lax.div(inside, SUBLANES) * (pieces * SUBLANES) + lax.rem(inside, SUBLANES)
             for p in range(pieces):
-                rows_ref[r : r + 1, p * LANES : (p + 1) * LANES] = bank_ref[block, tile + p, pl.ds(sub, 1), :]
-            level = bank_ref[block, last, 0:1, :]
+                rows_ref[r : r + 1, p * LANES : (p + 1) * LANES] = bank_ref[block, pl.ds(at + p * SUBLANES, 1), :]
+            level = bank_ref[block, last * SUBLANES : last * SUBLANES + 1, :]
             rows_ref[r : r + 1, taps : taps + LANES] = jnp.where(row_lane == inside, level, 0.0)
 
         @pl.when(jnp.logical_and(s >= 1, s <= sent_here))
@@ -699,7 +700,7 @@
         scratch_shapes=scratch()
         + [pltpu.VMEM(a.shape, a.dtype) for a in (fwd, inv, tw)]
         + [
-            pltpu.VMEM((n, tiles + 1, SUBLANES, LANES), jnp.float32),
+            pltpu.VMEM((n, (tiles + 1) * SUBLANES, LANES), jnp.float32),
             pltpu.VMEM((ROWS, taps + LANES), jnp.float32),
             pltpu.VMEM((ROWS // 2, length), jnp.float32),
             pltpu.SMEM(((1 + raws) * rows,), jnp.int32),
@@ -729,14 +730,15 @@
         out_specs=[hbm, smem],
         out_shape=[
             jax.ShapeDtypeStruct((rows, length), jnp.float32),
-            jax.ShapeDtypeStruct((kept * ROWS,), jnp.int32),
+            pltpu.SMEM((kept * ROWS,), jnp.int32),
         ],
         scratch_shapes=[dma],
         compiler_params=params,
     )(channel_order, came)
+    late_rows = pltpu.with_memory_space_constraint(late_rows, pltpu.SMEM)
     late = pl.pallas_call(
         functools.partial(late_kernel, n),
-        in_specs=[vmem, pl.BlockSpec(memory_space=pl.ANY)],
+        in_specs=[vmem, smem],
         out_specs=vmem,
         out_shape=pltpu.VMEM((kept, ROWS, length), jnp.float32),
         scratch_shapes=[dma((kept,)), dma((kept,))],

time: 187 us -> 186 us (level)
  no operation moved by 1% of the time
where the time goes in v5:
time: 186 us
  Pallas kernels  186 us (100%)
    pallas_call x1, Pallas kernels, local(): pl.pallas_call(functools.partial(exchange_kernel, n, taps), in_specs=[pl....  162 us
    pallas_call x1, Pallas kernels, local(): pl.pallas_call(functools.partial(late_kernel, n), in_specs=[vmem, smem],...  19.4 us

profile of v5, /device:TPU:16, one launch (start us, length us, event | category | flops | bytes accessed | tf_op | source)
XLA Modules:
  0.0 186.1 jit_solution(14128209117691252432)
XLA Ops:
  0.0 0.0 copy-start
  0.0 162.1 %shard_map.82.came_ref.buf_ref = f32[32,16,8192]{2,1,0:T(8,128)S(1)} custom-call(f32[256,8192]{1,0:T(8,128)} %x_ref.1, s32[256]{0:T(256)} %pick_ref.1, f32[16,256]{1,0:T(8,128)} %wave_ref.1, f32[16]{0:T(128)} %damp_ref.1, bf16[768,256]{1,0:T(8,128)(2,1)} %constant.6.clone.fwd_hbm, bf16[768,256]{1,0:T(8,128)(2,1)} %constant.7.clone.inv_hbm, ...), custom_call_target="tpu_custom_call" | custom-call | flops 3145728000 | bytes 16777216 | tf_op jit(solution)/shard_map/pallas_call | solution.py:695
  162.1 0.0 copy-done
  162.1 3.6 %shard_map.83 = (f32[256,8192]{1,0:T(8,128)}, s32[32]{0:T(128)S(4)}) custom-call(s32[256]{0:T(256)S(1)} %copy-done, f32[32,16,8192]{2,1,0:T(8,128)S(1)} %shard_map.82.came_ref.buf_ref), custom_call_target="tpu_custom_call" | custom-call | tf_op jit(solution)/shard_map/pallas_call | solution.py:727
  165.7 19.4 %shard_map.84.late_ref = f32[2,16,8192]{2,1,0:T(8,128)S(1)} custom-call(f32[32,16,8192]{2,1,0:T(8,128)S(1)} %shard_map.82.came_ref.buf_ref, s32[32]{0:T(128)S(4)} %get-tuple-element.7.after_ref.late_rows_ref), custom_call_target="tpu_custom_call" | custom-call | tf_op jit(solution)/shard_map/pallas_call | solution.py:739
  185.2 1.0 shard_map.85
Async XLA Ops:
  0.0 162.1 %copy-start = (s32[256]{0:T(256)S(1)}, s32[256]{0:T(256)}, u32[]{:S(2)}) copy-start(s32[256]{0:T(256)} %order_ref.1) | copy-start | bytes 3076

commit v6 on v5

--- a/solution.py
+++ b/solution.py
@@ -243,9 +243,7 @@
     kept = list(range(n - inner, n, 2))[1::-1]
     near = sorted(range(1, n // 2), key=lambda k: (k < inner, k))
     cross = [k for k in range(n // 2, n) if k not in raws + kept]
-    lead, rest = cross[:inner], cross[inner:]
-    mixed = lead[:1] + [k for pair in zip(lead[1:], near) for k in pair]
-    return mixed + near[max(len(lead) - 1, 0) :] + rest + kept + raws + [0], raws, kept
+    return cross + near + kept + raws + [0], raws, kept
 
 
 def keeps_blocks(me, n):

time: 186 us -> 186 us (level)
  no operation moved by 1% of the time
where the time goes in v6:
time: 186 us
  Pallas kernels  186 us (100%)
    pallas_call x1, Pallas kernels, local(): pl.pallas_call(functools.partial(exchange_kernel, n, taps), in_specs=[pl....  162 us
    pallas_call x1, Pallas kernels, local(): pl.pallas_call(functools.partial(late_kernel, n), in_specs=[vmem, smem],...  19.4 us

profile of v6, /device:TPU:16, one launch (start us, length us, event | category | flops | bytes accessed | tf_op | source)
XLA Modules:
  0.0 186.0 jit_solution(15175094196197214444)
XLA Ops:
  0.0 0.0 copy-start
  0.0 162.1 %shard_map.82.came_ref.buf_ref = f32[32,16,8192]{2,1,0:T(8,128)S(1)} custom-call(f32[256,8192]{1,0:T(8,128)} %x_ref.1, s32[256]{0:T(256)} %pick_ref.1, f32[16,256]{1,0:T(8,128)} %wave_ref.1, f32[16]{0:T(128)} %damp_ref.1, bf16[768,256]{1,0:T(8,128)(2,1)} %constant.6.clone.fwd_hbm, bf16[768,256]{1,0:T(8,128)(2,1)} %constant.7.clone.inv_hbm, ...), custom_call_target="tpu_custom_call" | custom-call | flops 3145728000 | bytes 16777216 | tf_op jit(solution)/shard_map/pallas_call | solution.py:693
  162.1 0.0 copy-done
  162.1 3.6 %shard_map.83 = (f32[256,8192]{1,0:T(8,128)}, s32[32]{0:T(128)S(4)}) custom-call(s32[256]{0:T(256)S(1)} %copy-done, f32[32,16,8192]{2,1,0:T(8,128)S(1)} %shard_map.82.came_ref.buf_ref), custom_call_target="tpu_custom_call" | custom-call | tf_op jit(solution)/shard_map/pallas_call | solution.py:725
  165.7 19.4 %shard_map.84.late_ref = f32[2,16,8192]{2,1,0:T(8,128)S(1)} custom-call(f32[32,16,8192]{2,1,0:T(8,128)S(1)} %shard_map.82.came_ref.buf_ref, s32[32]{0:T(128)S(4)} %get-tuple-element.7.after_ref.late_rows_ref), custom_call_target="tpu_custom_call" | custom-call | tf_op jit(solution)/shard_map/pallas_call | solution.py:737
  185.1 1.0 shard_map.85
Async XLA Ops:
  0.0 162.1 %copy-start = (s32[256]{0:T(256)S(1)}, s32[256]{0:T(256)}, u32[]{:S(2)}) copy-start(s32[256]{0:T(256)} %order_ref.1) | copy-start | bytes 3076

commit v7 on v6

--- a/solution.py
+++ b/solution.py
@@ -352,10 +352,7 @@
     stage = pl.ds(pl.multiple_of(partner * each, each // 2), each // 2)
     stage_in = pltpu.make_async_copy(x_ref.at[stage], stage_ref, stage_sem)
 
-    @pl.when(partner > me)
-    def _():
-        stage_in.start()
-
+    stage_in.start()
     lax.fori_loop(me + 1, n, greet, 0)
 
     @pl.when(me > 0)
@@ -365,7 +362,8 @@
     @pl.when(partner < me)
     def _():
         tell(ready_sems.at[me], partner)
-        raw(0, 0, False).start()
+        stage_in.wait()
+        raw_staged().start()
 
     damp_in = pltpu.make_async_copy(damp_ref, damp_smem, near_sems.at[0])
     pick_in = pltpu.make_async_copy(pick_ref, pick_smem.at[pl.ds(0, n * each)], near_sems.at[1])

time: 186 us -> 186 us (level)
  no operation moved by 1% of the time
where the time goes in v7:
time: 186 us
  Pallas kernels  186 us (100%)
    pallas_call x1, Pallas kernels, local(): pl.pallas_call(functools.partial(exchange_kernel, n, taps), in_specs=[pl....  162 us
    pallas_call x1, Pallas kernels, local(): pl.pallas_call(functools.partial(late_kernel, n), in_specs=[vmem, smem],...  19.6 us

profile of v7, /device:TPU:16, one launch (start us, length us, event | category | flops | bytes accessed | tf_op | source)
XLA Modules:
  0.0 186.0 jit_solution(17335166266912774038)
XLA Ops:
  0.0 0.0 copy-start
  0.0 161.9 %shard_map.82.came_ref.buf_ref = f32[32,16,8192]{2,1,0:T(8,128)S(1)} custom-call(f32[256,8192]{1,0:T(8,128)} %x_ref.1, s32[256]{0:T(256)} %pick_ref.1, f32[16,256]{1,0:T(8,128)} %wave_ref.1, f32[16]{0:T(128)} %damp_ref.1, bf16[768,256]{1,0:T(8,128)(2,1)} %constant.6.clone.fwd_hbm, bf16[768,256]{1,0:T(8,128)(2,1)} %constant.7.clone.inv_hbm, ...), custom_call_target="tpu_custom_call" | custom-call | flops 3145728000 | bytes 16777216 | tf_op jit(solution)/shard_map/pallas_call | solution.py:691
  161.9 0.0 copy-done
  161.9 3.6 %shard_map.83 = (f32[256,8192]{1,0:T(8,128)}, s32[32]{0:T(128)S(4)}) custom-call(s32[256]{0:T(256)S(1)} %copy-done, f32[32,16,8192]{2,1,0:T(8,128)S(1)} %shard_map.82.came_ref.buf_ref), custom_call_target="tpu_custom_call" | custom-call | tf_op jit(solution)/shard_map/pallas_call | solution.py:723
  165.5 19.6 %shard_map.84.late_ref = f32[2,16,8192]{2,1,0:T(8,128)S(1)} custom-call(f32[32,16,8192]{2,1,0:T(8,128)S(1)} %shard_map.82.came_ref.buf_ref, s32[32]{0:T(128)S(4)} %get-tuple-element.7.after_ref.late_rows_ref), custom_call_target="tpu_custom_call" | custom-call | tf_op jit(solution)/shard_map/pallas_call | solution.py:735
  185.1 1.0 shard_map.85
Async XLA Ops:
  0.0 161.9 %copy-start = (s32[256]{0:T(256)S(1)}, s32[256]{0:T(256)}, u32[]{:S(2)}) copy-start(s32[256]{0:T(256)} %order_ref.1) | copy-start | bytes 3076

commit v8 on v7

--- a/solution.py
+++ b/solution.py
@@ -240,7 +240,7 @@
 def block_order(n):
     inner = split_count(n)[1]
     raws = list(range(n - inner + 1, n, 2))[:2]
-    kept = list(range(n - inner, n, 2))[1::-1]
+    kept = list(range(n - inner, n, 2))[:2]
     near = sorted(range(1, n // 2), key=lambda k: (k < inner, k))
     cross = [k for k in range(n // 2, n) if k not in raws + kept]
     return cross + near + kept + raws + [0], raws, kept

time: 186 us -> 186 us (level)
  no operation moved by 1% of the time
where the time goes in v8:
time: 186 us
  Pallas kernels  186 us (100%)
    pallas_call x1, Pallas kernels, local(): pl.pallas_call(functools.partial(exchange_kernel, n, taps), in_specs=[pl....  162 us
    pallas_call x1, Pallas kernels, local(): pl.pallas_call(functools.partial(late_kernel, n), in_specs=[vmem, smem],...  19.7 us

profile of v8, /device:TPU:16, one launch (start us, length us, event | category | flops | bytes accessed | tf_op | source)
XLA Modules:
  0.0 186.1 jit_solution(17924230786999917485)
XLA Ops:
  0.0 0.0 copy-start
  0.0 161.9 %shard_map.82.came_ref.buf_ref = f32[32,16,8192]{2,1,0:T(8,128)S(1)} custom-call(f32[256,8192]{1,0:T(8,128)} %x_ref.1, s32[256]{0:T(256)} %pick_ref.1, f32[16,256]{1,0:T(8,128)} %wave_ref.1, f32[16]{0:T(128)} %damp_ref.1, bf16[768,256]{1,0:T(8,128)(2,1)} %constant.6.clone.fwd_hbm, bf16[768,256]{1,0:T(8,128)(2,1)} %constant.7.clone.inv_hbm, ...), custom_call_target="tpu_custom_call" | custom-call | flops 3145728000 | bytes 16777216 | tf_op jit(solution)/shard_map/pallas_call | solution.py:691
  161.9 0.0 copy-done
  161.9 3.6 %shard_map.83 = (f32[256,8192]{1,0:T(8,128)}, s32[32]{0:T(128)S(4)}) custom-call(s32[256]{0:T(256)S(1)} %copy-done, f32[32,16,8192]{2,1,0:T(8,128)S(1)} %shard_map.82.came_ref.buf_ref), custom_call_target="tpu_custom_call" | custom-call | tf_op jit(solution)/shard_map/pallas_call | solution.py:723
  165.5 19.7 %shard_map.84.late_ref = f32[2,16,8192]{2,1,0:T(8,128)S(1)} custom-call(f32[32,16,8192]{2,1,0:T(8,128)S(1)} %shard_map.82.came_ref.buf_ref, s32[32]{0:T(128)S(4)} %get-tuple-element.7.after_ref.late_rows_ref), custom_call_target="tpu_custom_call" | custom-call | tf_op jit(solution)/shard_map/pallas_call | solution.py:735
  185.1 1.0 shard_map.85
Async XLA Ops:
  0.0 161.9 %copy-start = (s32[256]{0:T(256)S(1)}, s32[256]{0:T(256)}, u32[]{:S(2)}) copy-start(s32[256]{0:T(256)} %order_ref.1) | copy-start | bytes 3076
